TPU v7x, 256 devices: a 2x2x32 block of a 4x8x32 slice. The times are simulated.
256 devices in a mesh: groups: 4 (over y, x), row: 32 (over z), col: 2 (over core).
Axes of the slice: x: 2, y: 2, z: 32, core: 2. Of those that a mesh axis runs over, the one named last changes fastest.
The devices are a block of a 4x8x32 slice.
Arguments:
- pair_rep: bfloat16 [1024, 256, 128], P(('groups', 'row'), 'col'), parts along dimension 0, may hold values from -6 to 6
- residue_mask: int32 [1024], P('groups'), parts along dimension 0, may hold values 0 or 1
- crop_length: int32 [4], P('groups'), parts along dimension 0, may hold values from 128 to 256
- norm_gain: float32 [2, 128], replicated, may hold values from 0.25 to 1.75
- mult_proj: bfloat16 [2, 128, 640], replicated, may hold values from -0.5 to 0.5
- mixed_gain: float32 [2, 128], replicated, may hold values from 0.25 to 1.75
- mult_out: bfloat16 [2, 128, 128], replicated, may hold values from -0.5 to 0.5
- att_gain: float32 [128], replicated, may hold values from 0.25 to 1.75
- att_proj: bfloat16 [128, 512], replicated, may hold values from -5 to 5
- att_bias: bfloat16 [128, 4], replicated, may hold values from -0.5 to 0.5
- att_out: bfloat16 [128, 128], replicated, may hold values from -0.5 to 0.5
Outputs:
- pair_out: bfloat16 [1024, 256, 128], P(('groups', 'row'), 'col'), parts along dimension 0
There are 4 independent parts, one for each index of `groups`. A program takes and returns all parts, laid end to end along the dimension named above; an argument that names none is the same for every part. Nothing has to cross between parts.
All inputs are finite; a program needn't handle non-finite values.
Results may differ from a plain program's by a relative error of at most 0.03.
Values may be sent and summed in bfloat16 or wider, within the bound.
A program may use at most 64 MiB of HBM per device.

v0:
```python
import jax
import jax.numpy as jnp
from jax import lax
from jax.sharding import PartitionSpec as P

HID = 128
HEADS = 4
HEAD_DIM = 32
ATT = 128


EPSILON = 1e-05


def normalize(values, gain_vec, along):
    average = jnp.mean(values, axis=along, keepdims=True)
    centered = values - average
    variance = jnp.mean(centered * centered, axis=along, keepdims=True)
    return centered * lax.rsqrt(variance + EPSILON) * gain_vec


def outgoing_product(left_half, right_half):
    return lax.dot_general(
        left_half,
        lax.all_gather(right_half, "row", axis=1, tiled=True),
        (((2,), (2,)), ((0,), (0,))),
        preferred_element_type=jnp.float32,
    )


def incoming_product(left_half, right_half):
    partial_value = lax.dot_general(
        left_half, right_half, (((1,), (1,)), ((0,), (0,))), preferred_element_type=jnp.float32
    )
    summed = lax.psum_scatter(
        jnp.transpose(partial_value, (1, 0, 2)).astype(jnp.bfloat16),
        "row",
        scatter_dimension=0,
        tiled=True,
    ).astype(jnp.float32)
    return jnp.transpose(summed, (1, 0, 2))


def triangle_update(pair_rep, gain_vec, proj_w, out_gain, out_w, pair_mask, incoming):
    normed = normalize(pair_rep.astype(jnp.float32), gain_vec, 2).astype(jnp.bfloat16)
    channels = jnp.einsum(
        "ijd,de->eij", normed, proj_w[:, : 4 * HID], preferred_element_type=jnp.float32
    )
    gate_lin = jnp.einsum(
        "ijd,de->ije", normed, proj_w[:, 4 * HID :], preferred_element_type=jnp.float32
    )
    masked = pair_mask[None, :, :]
    left_proj = (masked * jax.nn.sigmoid(channels[HID : 2 * HID]) * channels[:HID]).astype(
        jnp.bfloat16
    )
    right_proj = (
        masked * jax.nn.sigmoid(channels[3 * HID : 4 * HID]) * channels[2 * HID : 3 * HID]
    ).astype(jnp.bfloat16)
    left_half, right_half = (
        lax.all_to_all(left_proj, "col", split_axis=0, concat_axis=2, tiled=True),
        lax.all_to_all(right_proj, "col", split_axis=0, concat_axis=2, tiled=True),
    )
    if incoming:
        product = incoming_product(left_half, right_half)
    else:
        product = outgoing_product(left_half, right_half)
    mixed = product.astype(jnp.bfloat16)
    mixed_tile = lax.all_to_all(mixed, "col", split_axis=2, concat_axis=0, tiled=True)
    mixed_norm = normalize(mixed_tile.astype(jnp.float32), out_gain[:, None, None], 0).astype(
        jnp.bfloat16
    )
    update = jnp.einsum("cij,cd->ijd", mixed_norm, out_w, preferred_element_type=jnp.float32)
    return (pair_rep.astype(jnp.float32) + jax.nn.sigmoid(gate_lin) * update).astype(jnp.bfloat16)


def local(
    pair_rep,
    residue_mask,
    crop_length,
    norm_gain,
    mult_proj,
    mixed_gain,
    mult_out,
    att_gain,
    att_proj,
    att_bias,
    att_out,
):
    row_count = pair_rep.shape[0]
    col_count = pair_rep.shape[1]
    row_start = lax.axis_index("row") * row_count
    col_start = lax.axis_index("col") * col_count
    positions = jnp.arange(residue_mask.shape[0], dtype=jnp.int32)
    alive = (((residue_mask == 1) | (positions == 0)) & (positions < crop_length[0])).astype(
        jnp.float32
    )
    row_alive = lax.dynamic_slice_in_dim(alive, row_start, row_count, 0)
    col_alive = lax.dynamic_slice_in_dim(alive, col_start, col_count, 0)
    pair_mask = row_alive[:, None] * col_alive[None, :]
    first = triangle_update(
        pair_rep, norm_gain[0], mult_proj[0], mixed_gain[0], mult_out[0], pair_mask, False
    )
    second = triangle_update(
        first, norm_gain[1], mult_proj[1], mixed_gain[1], mult_out[1], pair_mask, True
    )
    normed = normalize(second.astype(jnp.float32), att_gain, 2).astype(jnp.bfloat16)
    projected = jnp.einsum("ijd,de->ije", normed, att_proj, preferred_element_type=jnp.float32)
    queries = projected[..., :ATT].astype(jnp.bfloat16)
    key_rows = projected[..., ATT : 2 * ATT].astype(jnp.bfloat16)
    value_rows = projected[..., 2 * ATT : 3 * ATT].astype(jnp.bfloat16)
    gates = projected[..., 3 * ATT :].astype(jnp.bfloat16)
    bias_tile = jnp.einsum(
        "ijd,dh->hij", normed, att_bias, preferred_element_type=jnp.float32
    ).astype(jnp.bfloat16)
    key_all, value_all, bias_cols = (
        lax.all_gather(key_rows, "col", axis=1, tiled=True),
        lax.all_gather(value_rows, "col", axis=1, tiled=True),
        lax.all_gather(bias_tile, "col", axis=2, tiled=True),
    )
    bias_full = lax.all_gather(bias_cols, "row", axis=1, tiled=True)
    bias_mine = lax.dynamic_slice_in_dim(bias_full, col_start, col_count, 1).astype(jnp.float32)
    total = key_all.shape[1]
    key_mask = jnp.where(alive > 0, 0.0, -1000000000.0).astype(jnp.float32)
    scaling = 1.0 / float(HEAD_DIM) ** 0.5
    query_heads = queries.reshape(row_count, col_count, HEADS, HEAD_DIM)
    key_heads = key_all.reshape(row_count, total, HEADS, HEAD_DIM)
    value_heads = value_all.reshape(row_count, total, HEADS, HEAD_DIM)
    scores = jnp.einsum(
        "ijhd,ikhd->hijk", query_heads, key_heads, preferred_element_type=jnp.float32
    )
    scores = scores * scaling + bias_mine[:, None, :, :] + key_mask[None, None, None, :]
    weights = jax.nn.softmax(scores, axis=-1).astype(jnp.bfloat16)
    attended = jnp.einsum(
        "hijk,ikhd->ijhd", weights, value_heads, preferred_element_type=jnp.float32
    )
    attended = attended.reshape(row_count, col_count, ATT)
    gated = (jax.nn.sigmoid(gates.astype(jnp.float32)) * attended).astype(jnp.bfloat16)
    result = jnp.einsum("ija,ad->ijd", gated, att_out, preferred_element_type=jnp.float32)
    return (second.astype(jnp.float32) + result).astype(jnp.bfloat16)


def solution(mesh):
    placed = (
        P(("groups", "row"), "col", None),
        P("groups"),
        P("groups"),
        P(),
        P(),
        P(),
        P(),
        P(),
        P(),
        P(),
        P(),
    )
    return jax.shard_map(
        local,
        mesh=mesh,
        in_specs=placed,
        out_specs=P(("groups", "row"), "col", None),
        check_vma=False,
    )
```

profile of v0, /device:TPU:46, one launch (start us, length us, event | category | flops | bytes accessed | tf_op | source)
XLA Modules:
  0.0 475.7 jit_solution(16290385948561313157)
XLA Ops:
  6.6 1.2 copy.297
  7.9 1.0 fusion.83
  9.1 0.8 slice_bitcast_fusion.8
  10.5 0.7 compare_select_fusion
  11.4 0.5 convolution_bitcast_fusion.1
  12.5 4.0 all_to_all.90
  16.4 0.7 copy.397
  17.2 0.9 copy.302
  18.1 3.5 all-to-all-start
  22.3 0.8 all-to-all-done
  23.1 190.0 %all-gather.2.cloned.1.call-done = bf16[64,256,256]{2,1,0:T(8,128)(2,1)} async-done(((bf16[64,8,256]{2,1,0:T(8,128)(2,1)}), bf16[64,256,256]{2,1,0:T(8,128)(2,1)}) %all-gather.2.cloned.1.call-update) | async-done | bytes 8388624 | tf_op jit(solution)/shard_map/all_gather | solution.py:25
  213.1 5.6 %convolution_convert_fusion.1 = bf16[64,8,256]{2,1,0:T(8,128)(2,1)S(1)} fusion(bf16[64,256,256]{2,1,0:T(8,128)(2,1)} %all-gather.2.cloned.1.call-done, bf16[64,8,2,128]{3,1,0,2:T(8,128)(2,1)S(1)} %bitcast.147), kind=kOutput, calls=%fused_computation.32 | convolution fusion | flops 67239936 | bytes 8912896 | tf_op jit(solution)/shard_map/dot_general | solution.py:23
  219.6 4.0 all_to_all.91
  225.2 0.5 convolution_bitcast_fusion
  226.1 0.9 copy.320
  227.0 3.5 all-to-all-start.3
  230.7 1.3 all-to-all-done.3
  232.0 3.9 all_to_all.92
  235.9 5.6 %convert_bitcast_fusion = bf16[64,32,8,256]{3,2,1,0:T(8,128)(2,1)} fusion(bf16[64,8,2,128]{3,1,0,2:T(8,128)(2,1)S(1)} %bitcast.151, bf16[64,8,2,128]{3,1,0,2:T(8,128)(2,1)S(1)} %bitcast.148), kind=kOutput, calls=%fused_computation.1 | convolution fusion | flops 71303168 | bytes 8912896 | tf_op jit(solution)/shard_map/dot_general | solution.py:32
  241.5 7.6 %copy.368 = bf16[64,32,8,256]{3,2,0,1:T(8,128)(2,1)} copy(bf16[64,32,8,256]{3,2,1,0:T(8,128)(2,1)} %convert_bitcast_fusion) | data formatting | bytes 16777216
  249.8 143.4 %reduce-scatter.4.cloned.1.call-done = bf16[8,16384]{1,0:T(8,128)(2,1)} async-done(((bf16[256,16384]{1,0:T(8,128)(2,1)}), bf16[8,16384]{1,0:T(8,128)(2,1)}) %reduce-scatter.4.cloned.1.call-update) | async-done | bytes 262160
  393.2 1.4 copy.324
  395.1 4.0 all_to_all.93
  401.0 1.8 all_gather.18
  402.8 55.3 %all_gather.19 = bf16[4,256,256]{2,0,1:T(4,128)(2,1)S(1)} all-gather(bf16[4,8,256]{2,0,1:T(4,128)(2,1)S(1)} %all_gather.18), channel_id=1, replica_groups=mesh['groups'=4,'row'=32,'col'=2] {'row'}, dimensions={1}, use_global_device_ids=true | all-gather | bytes 540672 | tf_op jit(solution)/shard_map/all_gather | solution.py:120
  458.2 0.5 convolution_convert_fusion
  458.8 2.3 all_gather.17
  461.1 2.2 all_gather.16
  463.3 0.8 fusion.61
  464.1 2.0 fusion.86
  466.1 1.5 fusion.2
  468.0 0.9 copy.343
  (69 shorter events, 8.3 us)
Async XLA Ops:
  6.5 451.7 %copy-start = (bf16[128,512]{1,0:T(8,128)(2,1)S(1)}, bf16[128,512]{1,0:T(8,128)(2,1)}, u32[]{:S(2)}) copy-start(bf16[128,512]{1,0:T(8,128)(2,1)} %param.19) | copy-start | bytes 393220
  6.6 206.6 %all-gather.2.cloned.1.call-start = ((), (), s32[]{:S(2)}) async-start(), calls=%async_computation.7 | async-start | bytes 8650752 | tf_op jit(solution)/shard_map/all_gather | solution.py:25
  8.9 12.7 %copy-start.5 = (f32[2,128]{1,0:T(2,128)S(1)}, f32[2,128]{1,0:T(2,128)}, u32[]{:S(2)}) copy-start(f32[2,128]{1,0:T(2,128)} %param.16) | copy-start | bytes 3076
  18.1 5.0 %all-to-all-start = ((bf16[128,8,128]{2,1,0:T(8,128)(2,1)}), bf16[128,8,128]{2,1,0:T(8,128)(2,1)S(1)}, u32[]{:S(2)}, u32[]{:S(2)}) async-start(bf16[128,8,128]{2,1,0:T(8,128)(2,1)} %copy.302), calls=%async_computation | async-start | bytes 524288 | tf_op jit(solution)/shard_map/all_to_all | solution.py:60
  218.7 6.1 %copy-start.1 = (bf16[2,128,128]{2,1,0:T(8,128)(2,1)S(1)}, bf16[2,128,128]{2,1,0:T(8,128)(2,1)}, u32[]{:S(2)}) copy-start(bf16[2,128,128]{2,1,0:T(8,128)(2,1)} %param.17) | copy-start | bytes 196612
  227.0 5.0 %all-to-all-start.3 = ((bf16[128,8,128]{2,1,0:T(8,128)(2,1)}), bf16[128,8,128]{2,1,0:T(8,128)(2,1)S(1)}, u32[]{:S(2)}, u32[]{:S(2)}) async-start(bf16[128,8,128]{2,1,0:T(8,128)(2,1)} %copy.320), calls=%async_computation.3 | async-start | bytes 524288 | tf_op jit(solution)/shard_map/all_to_all | solution.py:60
  230.5 162.7 %reduce-scatter.4.cloned.1.call-start = ((), (), s32[]{:S(2)}) async-start(), calls=%async_computation.8 | async-start | bytes 8650752
  249.8 150.9 %copy-start.3 = (f32[128]{0:T(128)S(1)}, f32[128]{0:T(128)}, u32[]{:S(2)}) copy-start(f32[128]{0:T(128)} %param.18) | copy-start | bytes 1540
  249.8 150.9 %copy-start.4 = (bf16[128,4]{0,1:T(4,128)(2,1)S(1)}, bf16[128,4]{0,1:T(4,128)(2,1)}, u32[]{:S(2)}) copy-start(bf16[128,4]{0,1:T(4,128)(2,1)} %param.20) | copy-start | bytes 3076
  466.1 1.7 copy-start.2
Sparse Core Ops, SparseCore 0:
  17.4 195.7 all-gather.1
  249.4 143.8 reduce-scatter.3
where the time goes:
time: 478 us; the launch traced here: 476 us
  waiting for transfers between devices  336 us (70%)
  blocking collectives  77.5 us (16%)
  local copies, waits for them, and re-layouts  19.6 us (4%)
  matrix products  16.8 us (4%)
  between operations  14.5 us (3%)
  starting transfers between devices  7.01 us (1%)
  other arithmetic  4.83 us (1%)
    all_gather x1, waiting for transfers between devices, outgoing_product(): lax.all_gather(right_half, 'row', axis=1, tiled=True)  190 us
    unnamed x3, waiting for transfers between devices  144 us
    all_gather x1, blocking collectives, local(): bias_full = lax.all_gather(bias_cols, 'row', axis=1, tiled=True)  55.3 us
    unnamed x20, local copies, waits for them, and re-layouts  10.6 us
  transfers between devices with their start and end apart: 4, of which 4 were waited for; matrix products, arithmetic and copies ran while one was open for 0% of the time, Pallas kernels for 0%

commit v1 on v0

v1 whole, which is shorter than its diff:
```python
import functools

import jax
import jax.numpy as jnp
from jax import lax
from jax.experimental import pallas as pl
from jax.experimental.pallas import tpu as pltpu
from jax.sharding import PartitionSpec as P

HEADS = 4
EPSILON = 1e-05
MESH = pl.DeviceIdType.MESH
F32 = jnp.float32
BF16 = jnp.bfloat16
NN = (((1,), (0,)), ((), ()))
NT = (((1,), (1,)), ((), ()))
TN = (((0,), (0,)), ((), ()))


def dot(a, b, dims):
    return lax.dot_general(a, b, dims, preferred_element_type=F32)


def norm_lanes(v, gain):
    mean = jnp.mean(v, axis=-1, keepdims=True)
    cen = v - mean
    var = jnp.mean(cen * cen, axis=-1, keepdims=True)
    return cen * lax.rsqrt(var + EPSILON) * gain


def norm_sublanes(v, gain):
    mean = jnp.mean(v, axis=0, keepdims=True)
    cen = v - mean
    var = jnp.mean(cen * cen, axis=0, keepdims=True)
    return cen * lax.rsqrt(var + EPSILON) * gain


def kernel(
    nz, nc, rows, x_ref, pm_ref, km_ref, ng_ref, mp_ref, mg_ref, mo_ref, ag_ref, ap_ref, ab_ref, ao_ref,
    out_ref,
    wt, mgt, apt, abt, nrm, gate, zb, fl, fr, s_lr, r_lr, s_p, r_p, nall, fb, s_b, r_b, bt, sc, vt, sg,
    sem_lr_s, sem_lr_r, sem_p_s, sem_p_r, sem_n, sem_b,
):
    z = lax.axis_index("row")
    c = lax.axis_index("col")
    me = z * nc + c
    devs = nz * nc
    cols = pm_ref.shape[1]
    ch = x_ref.shape[1]
    per = s_lr.shape[0]
    block = devs * rows
    half = nz // 2
    other = 1 - c

    barrier = pltpu.get_barrier_semaphore()

    def greet(t, carry):
        zz = lax.rem(z + t, nz)
        for cc in range(nc):
            pl.semaphore_signal(barrier, inc=1, device_id={"row": zz, "col": cc}, device_id_type=MESH)
        return carry

    pl.semaphore_signal(barrier, inc=1, device_id={"row": z, "col": other}, device_id_type=MESH)
    lax.fori_loop(1, nz, greet, 0)

    def remote(src, dst, ssem, rsem, zz, cc):
        return pltpu.make_async_remote_copy(
            src_ref=src, dst_ref=dst, send_sem=ssem, recv_sem=rsem,
            device_id={"row": zz, "col": cc}, device_id_type=MESH,
        )

    def far_first(step):
        d = half - (step + 1) // 2
        off = jnp.where(lax.rem(step, 2) == 1, d, nz - d)
        return lax.rem(z + off, nz)

    def scatter(src_at, dst, ssem, rsem):
        def one(step, carry):
            zz = far_first(step)
            for cc in range(nc):
                to = lax.rem(c + cc, nc)
                remote(src_at(zz, to), dst, ssem, rsem, zz, to).start()
            return carry

        lax.fori_loop(0, nz - 1, one, 0)
        remote(src_at(z, other), dst, ssem, rsem, z, other).start()

    def landed(buf, ssem, rsem):
        every = buf.at[pl.ds(0, devs - 1)]
        return remote(every, every, ssem, rsem, z, other)

    for u in range(2):
        for q in range(4):
            wt[u, q * ch:(q + 1) * ch, :] = jnp.transpose(
                mp_ref[u, :, q * ch:(q + 1) * ch].astype(F32)).astype(BF16)
        mgt[u] = jnp.transpose(jnp.broadcast_to(mg_ref[u:u + 1, :], (ch, ch)))

    def project(u, r):
        sl = pl.ds(pl.multiple_of(r * cols, cols), cols)
        src = x_ref if u == 0 else zb
        normed = norm_lanes(src[sl, :].astype(F32), ng_ref[u:u + 1, :]).astype(BF16)
        nrm[sl, :] = normed
        pt = dot(wt[u], normed, NT)
        mask = pm_ref[pl.ds(r, 1), :]
        left = mask * jax.nn.sigmoid(pt[ch:2 * ch]) * pt[:ch]
        right = mask * jax.nn.sigmoid(pt[3 * ch:]) * pt[2 * ch:3 * ch]
        fl[pl.ds(r, ch, stride=rows), :] = left
        fr[pl.ds(r, ch, stride=rows), :] = right

    def send_lr(u, k):
        pair = jnp.concatenate(
            [
                fl[k * block:(k + 1) * block, :].reshape(devs, rows, cols),
                fr[k * block:(k + 1) * block, :].reshape(devs, rows, cols),
            ],
            axis=1,
        )
        s_lr[k] = pair.astype(BF16)
        r_lr[u, k, c * nz + z] = s_lr[k, me]
        scatter(
            lambda zz, cc: s_lr.at[k, zz * nc + cc], r_lr.at[u, k, c * nz + z],
            sem_lr_s.at[k], sem_lr_r.at[u, k])

    def gate_row(u):
        def one(r, carry):
            sl = pl.ds(pl.multiple_of(r * cols, cols), cols)
            gate[sl, :] = jax.nn.sigmoid(dot(nrm[sl, :], mp_ref[u, :, 4 * ch:], NN))
            return carry

        lax.fori_loop(0, rows, one, 0)

    def product(u, k):
        wait = landed(r_lr.at[u, k], sem_lr_s.at[k], sem_lr_r.at[u, k])
        wait.wait_recv()
        lefts, rights = [], []
        for cc in range(nc):
            part = r_lr[u, k, cc * nz:(cc + 1) * nz].astype(F32)
            lefts.append(part[:, :rows].reshape(nz * rows, cols).astype(BF16))
            rights.append(part[:, rows:].reshape(nz * rows, cols).astype(BF16))
        left = jnp.concatenate(lefts, axis=1)
        right = jnp.concatenate(rights, axis=1)
        prod = dot(left, right, NT if u == 0 else TN)
        for cc in range(nc):
            s_p[k, cc] = prod[:, cc * cols:(cc + 1) * cols].reshape(nz, rows, cols).astype(BF16)
        r_p[u, k, me] = s_p[k, c, z]
        scatter(lambda zz, cc: s_p.at[k, cc, zz], r_p.at[u, k, me], sem_p_s.at[k], sem_p_r.at[u, k])
        wait.wait_send()

    def updated(u, r):
        sl = pl.ds(pl.multiple_of(r * cols, cols), cols)
        mixed = norm_sublanes(fl[pl.ds(r, ch, stride=rows), :], mgt[u]).astype(BF16)
        upd = dot(mixed, mo_ref[u], TN)
        src = x_ref if u == 0 else zb
        zb[sl, :] = (src[sl, :].astype(F32) + gate[sl, :] * upd).astype(BF16)

    def rows_loop(f):
        def one(r, carry):
            f(r)
            return carry

        lax.fori_loop(0, rows, one, 0)

    for u in range(2):
        rows_loop(functools.partial(project, u))
        if u == 0:
            pl.semaphore_wait(barrier, devs - 1)
        for k in range(per):
            send_lr(u, k)
        gate_row(u)
        if u == 0:
            for q in range(4):
                apt[q * ch:(q + 1) * ch, :] = jnp.transpose(
                    ap_ref[:, q * ch:(q + 1) * ch].astype(F32)).astype(BF16)
            abt[...] = jnp.transpose(ab_ref[...].astype(F32)).astype(BF16)
        for k in range(per):
            product(u, k)
        for k in range(per):
            wait = landed(r_p.at[u, k], sem_p_s.at[k], sem_p_r.at[u, k])
            wait.wait_recv()
            fl[k * block:(k + 1) * block, :] = r_p[u, k].astype(F32).reshape(block, cols)
            wait.wait_send()
        rows_loop(functools.partial(updated, u))

    def normed_row(r):
        sl = pl.ds(pl.multiple_of(r * cols, cols), cols)
        normed = norm_lanes(zb[sl, :].astype(F32), ag_ref[...]).astype(BF16)
        nall[c, sl, :] = normed
        fb[pl.ds(r, abt.shape[0], stride=rows), :] = dot(abt[...], normed, NT)

    rows_loop(normed_row)
    hr = HEADS * rows
    s_b[...] = fb[:hr, :].astype(BF16)
    mine = lax.rem(z, half)
    to = z // half

    def spread(step, carry):
        zz = far_first(step)
        remote(s_b, r_b.at[c * half + mine], sem_b.at[0], sem_b.at[1], zz, to).start()
        return carry

    lax.fori_loop(0, nz - 1, spread, 0)

    @pl.when(to == c)
    def _():
        r_b[c * half + mine] = s_b[...]

    @pl.when(to != c)
    def _():
        remote(s_b, r_b.at[c * half + mine], sem_b.at[0], sem_b.at[1], z, other).start()

    swap = remote(nall.at[c], nall.at[c], sem_n.at[0], sem_n.at[1], z, other)
    swap.start()
    swap.wait()

    def scores_row(r):
        sl = pl.ds(pl.multiple_of(r * cols, cols), cols)
        mine_n = nall[c, sl, :]
        full = jnp.concatenate([nall[cc, sl, :] for cc in range(nc)], axis=0)
        qt = dot(apt[:ch], mine_n, NT).astype(BF16)
        gt = dot(apt[3 * ch:], mine_n, NT).astype(BF16)
        keys = dot(full, ap_ref[:, ch:2 * ch], NN).astype(BF16)
        vt[r] = dot(apt[2 * ch:3 * ch], full, NT).astype(BF16)
        sg[r] = jax.nn.sigmoid(gt.astype(F32))
        hd = ch // HEADS
        wide = []
        for h in range(HEADS):
            parts = [jnp.zeros((h * hd, cols), BF16)] if h else []
            parts.append(qt[h * hd:(h + 1) * hd])
            if h < HEADS - 1:
                parts.append(jnp.zeros(((HEADS - 1 - h) * hd, cols), BF16))
            wide.append(jnp.concatenate(parts, axis=0))
        sc[r] = dot(keys, jnp.concatenate(wide, axis=1), NN)

    rows_loop(scores_row)

    def bias_wait(count):
        return remote(r_b.at[pl.ds(0, count)], r_b.at[pl.ds(0, count)], sem_b.at[0], sem_b.at[1], z, other)

    @pl.when(to == c)
    def _():
        bias_wait(nz - 1).wait()

    @pl.when(to != c)
    def _():
        bias_wait(nz).wait()

    for kc in range(nc):
        part = r_b[kc * half:(kc + 1) * half].astype(F32)
        for h in range(HEADS):
            tile = part[:, h * rows:(h + 1) * rows].reshape(half * rows, cols) + km_ref[kc:kc + 1, :]
            bt[kc * cols:(kc + 1) * cols, h * cols:(h + 1) * cols] = jnp.transpose(tile)

    hd = ch // HEADS
    scale = 1.0 / float(hd) ** 0.5

    def attend_row(r):
        sl = pl.ds(pl.multiple_of(r * cols, cols), cols)
        score = sc[r] * scale + bt[...]
        top = jnp.max(score, axis=0, keepdims=True)
        e = jnp.exp(score - top)
        inv = 1.0 / jnp.sum(e, axis=0, keepdims=True)
        got = dot(vt[r], e.astype(BF16), NN)
        parts = []
        for h in range(HEADS):
            lanes = slice(h * cols, (h + 1) * cols)
            parts.append(got[h * hd:(h + 1) * hd, lanes] * inv[:, lanes])
        gated = (sg[r] * jnp.concatenate(parts, axis=0)).astype(BF16)
        out_ref[sl, :] = (zb[sl, :].astype(F32) + dot(gated, ao_ref[...], TN)).astype(BF16)

    rows_loop(attend_row)


def solution(mesh):
    nz, nc = mesh.shape["row"], mesh.shape["col"]
    devs = nz * nc

    def local(pair_rep, residue_mask, crop_length, norm_gain, mult_proj, mixed_gain, mult_out, att_gain, att_proj,
              att_bias, att_out):
        rows, cols, ch = pair_rep.shape
        per = ch // devs
        half = nz // 2
        z, c = lax.axis_index("row"), lax.axis_index("col")
        positions = jnp.arange(residue_mask.shape[0], dtype=jnp.int32)
        alive = (((residue_mask == 1) | (positions == 0)) & (positions < crop_length[0])).astype(F32)
        row_alive = lax.dynamic_slice_in_dim(alive, z * rows, rows, 0)
        col_alive = lax.dynamic_slice_in_dim(alive, c * cols, cols, 0)
        pair_mask = row_alive[:, None] * col_alive[None, :]
        key_mask = jnp.where(alive > 0, 0.0, -1000000000.0).astype(F32).reshape(nc, cols)
        area = rows * cols
        vmem = pltpu.VMEM
        out = pl.pallas_call(
            functools.partial(kernel, nz, nc, rows),
            out_shape=jax.ShapeDtypeStruct((area, ch), BF16),
            in_specs=[pl.BlockSpec(memory_space=vmem)] * 11,
            out_specs=pl.BlockSpec(memory_space=vmem),
            scratch_shapes=[
                vmem((2, 4 * ch, ch), BF16),
                vmem((2, ch, ch), F32),
                vmem((4 * ch, ch), BF16),
                vmem((HEADS, ch), BF16),
                vmem((area, ch), BF16),
                vmem((area, ch), F32),
                vmem((area, ch), BF16),
                vmem((ch * rows, cols), F32),
                vmem((ch * rows, cols), F32),
                vmem((per, devs, 2 * rows, cols), BF16),
                vmem((2, per, devs, 2 * rows, cols), BF16),
                vmem((per, nc, nz, rows, cols), BF16),
                vmem((2, per, devs, rows, cols), BF16),
                vmem((nc, area, ch), BF16),
                vmem((HEADS * rows, cols), F32),
                vmem((HEADS * rows, cols), BF16),
                vmem((nc * half, HEADS * rows, cols), BF16),
                vmem((nc * cols, HEADS * cols), F32),
                vmem((rows, nc * cols, HEADS * cols), F32),
                vmem((rows, ch, nc * cols), BF16),
                vmem((rows, ch, cols), F32),
                pltpu.SemaphoreType.DMA((per,)),
                pltpu.SemaphoreType.DMA((2, per)),
                pltpu.SemaphoreType.DMA((per,)),
                pltpu.SemaphoreType.DMA((2, per)),
                pltpu.SemaphoreType.DMA((2,)),
                pltpu.SemaphoreType.DMA((2,)),
            ],
            compiler_params=pltpu.CompilerParams(
                collective_id=1, has_side_effects=True, vmem_limit_bytes=48 * 1024 * 1024
            ),
            name="triangle",
        )(
            pair_rep.reshape(area, ch), pair_mask, key_mask, norm_gain, mult_proj, mixed_gain, mult_out,
            att_gain.reshape(1, ch), att_proj, att_bias, att_out,
        )
        return out.reshape(rows, cols, ch)

    return jax.shard_map(
        local,
        mesh=mesh,
        in_specs=(P(("groups", "row"), "col", None), P("groups"), P("groups")) + (P(),) * 8,
        out_specs=P(("groups", "row"), "col", None),
        check_vma=False,
    )
```

time: 478 us -> 224 us (0.47)
  waiting for transfers between devices: 336 us -> 0 us
  Pallas kernels: 0 us -> 216 us
  blocking collectives: 77.5 us -> 0 us
  matrix products: 16.8 us -> 0 us
  local copies, waits for them, and re-layouts: 19.6 us -> 5.3 us
  between operations: 14.5 us -> 0.73 us
  starting transfers between devices: 7.01 us -> 0 us
    pallas_call x0 -> x1, Pallas kernels: none -> 216 us  [local(): pl.pallas_call(functools.partial(kernel, nz, nc, rows), out_shape=jax.Sha...]
    all_gather x1 -> x0, waiting for transfers between devices: 190 us -> none  [outgoing_product(): lax.all_gather(right_half, 'row', axis=1, tiled=True)]
    unnamed x3 -> x0, waiting for transfers between devices: 144 us -> none
    all_gather x4 -> x0, blocking collectives: 61.6 us -> none  [the longest x1 55.3 us: local(): bias_full = lax.all_gather(bias_cols, 'row', axis=1, tiled=True)]
    dot_general x13 -> x0, matrix products: 16.8 us -> none  [the longest x1 5.64 us: outgoing_product(): lax.dot_general(left_half, lax.all_gather(right_half, 'row', axis=1, tile...]
    all_to_all x4 -> x0, blocking collectives: 15.8 us -> none  [the longest x2 7.92 us: triangle_update(): lax.all_to_all(mixed, 'col', split_axis=2, concat_axis=0, tiled=True)]
    all_to_all x2 -> x0, starting transfers between devices: 6.94 us -> none  [triangle_update(): lax.all_to_all(left_proj, 'col', split_axis=0, concat_axis=2, tiled=True)]
    unnamed x20 -> x18, local copies, waits for them, and re-layouts: 10.6 us -> 5.15 us
  transfers between devices with their start and end apart: 4 -> 0, of which waited for: 4 -> 0; matrix products, arithmetic and copies ran while one was open for 0% -> 0% of each run, Pallas kernels for 0% -> 0%
where the time goes in v1:
time: 224 us; the launch traced here: 223 us
  Pallas kernels  216 us (96%)
  local copies, waits for them, and re-layouts  5.3 us (2%)
    pallas_call x1, Pallas kernels, local(): pl.pallas_call(functools.partial(kernel, nz, nc, rows), out_shape=jax.Sha...  216 us
    unnamed x18, local copies, waits for them, and re-layouts  5.15 us

profile of v1, /device:TPU:46, one launch (start us, length us, event | category | flops | bytes accessed | tf_op | source)
XLA Modules:
  0.0 222.9 jit_solution(18179535025789881052)
XLA Ops:
  0.0 0.0 copy-start.3
  0.7 0.7 fusion
  1.4 0.1 dynamic_slice.7
  1.4 0.1 dynamic_slice.6
  1.5 0.1 broadcast_multiply_fusion.pm_ref
  1.6 0.0 copy-start.5
  1.6 0.0 copy-start.6
  1.6 0.0 copy-start.7
  1.6 0.8 copy.12.ab_ref
  2.5 0.0 copy-done.3
  2.5 0.0 copy-done.5
  2.5 0.0 copy-done.6
  2.5 0.0 copy-done.7
  2.5 0.0 copy-start
  2.5 1.0 copy-done
  3.5 0.0 copy-start.1
  3.5 0.9 copy-done.1
  4.4 0.0 copy-start.2
  4.4 0.9 copy-done.2
  5.3 0.0 copy-start.4
  5.3 0.8 copy-done.4
  6.1 216.2 %triangle.1 = bf16[1024,128]{1,0:T(8,128)(2,1)S(1)} custom-call(bf16[1024,128]{1,0:T(8,128)(2,1)S(1)} %bitcast.8, f32[8,128]{1,0:T(8,128)S(1)} %broadcast_multiply_fusion.pm_ref, f32[2,128]{1,0:T(2,128)S(1)} %get-tuple-element.5.km_ref, f32[2,128]{1,0:T(2,128)S(1)} %copy-done.5, bf16[2,128,640]{2,1,0:T(8,128)(2,1)S(1)} %copy-done, f32[2,128]{1,0:T(2,128)S(1)} %copy-done.6, ...), custom_call_target="tpu_custom_call" | custom-call | tf_op jit(solution)/shard_map/triangle/pallas_call | solution.py:291
  222.2 0.7 copy.15
Async XLA Ops:
  0.0 2.5 %copy-start.3 = (bf16[2,128,128]{2,1,0:T(8,128)(2,1)S(1)}, bf16[2,128,128]{2,1,0:T(8,128)(2,1)}, u32[]{:S(2)}) copy-start(bf16[2,128,128]{2,1,0:T(8,128)(2,1)} %mo_ref.1) | copy-start | bytes 196612
  1.6 0.9 copy-start.5
  1.6 0.9 copy-start.6
  1.6 0.9 copy-start.7
  2.5 1.0 copy-start
  3.5 0.9 copy-start.1
  4.4 0.9 copy-start.2
  5.3 0.8 copy-start.4

commit v2 on v1

--- a/solution.py
+++ b/solution.py
@@ -36,10 +36,11 @@
 
 
 def kernel(
-    nz, nc, rows, x_ref, pm_ref, km_ref, ng_ref, mp_ref, mg_ref, mo_ref, ag_ref, ap_ref, ab_ref, ao_ref,
+    nz, nc, rows, stride, crop_ref, rm_hbm, x_hbm, ng_hbm, mp_hbm, mg_hbm, mo_hbm, ag_hbm, ap_hbm, ab_hbm, ao_hbm,
     out_ref,
-    wt, mgt, apt, abt, nrm, gate, zb, fl, fr, s_lr, r_lr, s_p, r_p, nall, fb, s_b, r_b, bt, sc, vt, sg,
-    sem_lr_s, sem_lr_r, sem_p_s, sem_p_r, sem_n, sem_b,
+    rm_ref, x_ref, ng_ref, mp_ref, mg_ref, mo_ref, ag_ref, ap_ref, ab_ref, ao_ref, sem_in,
+    pm_ref, km_ref, wt, mgt, apt, nrm, gate, zb, fl, fr, s_lr, r_lr, s_p, r_p, nall, fb, s_b, r_b, bt, sc, vt, sg,
+    level, sem_lr_s, sem_lr_r, sem_p_s, sem_p_r, sem_n, sem_b,
 ):
     z = lax.axis_index("row")
     c = lax.axis_index("col")
@@ -54,14 +55,27 @@
 
     barrier = pltpu.get_barrier_semaphore()
 
-    def greet(t, carry):
-        zz = lax.rem(z + t, nz)
-        for cc in range(nc):
-            pl.semaphore_signal(barrier, inc=1, device_id={"row": zz, "col": cc}, device_id_type=MESH)
-        return carry
-
-    pl.semaphore_signal(barrier, inc=1, device_id={"row": z, "col": other}, device_id_type=MESH)
-    lax.fori_loop(1, nz, greet, 0)
+    left, right = lax.rem(z + nz - 1, nz), lax.rem(z + 1, nz)
+    for zz, cc in ((left, c), (right, c), (z, other)):
+        pl.semaphore_signal(barrier, inc=1, device_id={"row": zz, "col": cc}, device_id_type=MESH)
+    loads = []
+    for i, (src, dst) in enumerate((
+        (x_hbm, x_ref), (ng_hbm, ng_ref), (mp_hbm, mp_ref), (rm_hbm, rm_ref), (mg_hbm, mg_ref), (mo_hbm, mo_ref),
+        (ag_hbm, ag_ref), (ap_hbm, ap_ref), (ab_hbm, ab_ref), (ao_hbm, ao_ref),
+    )):
+        loads.append(pltpu.make_async_copy(src, dst, sem_in.at[i]))
+        loads[-1].start()
+
+    def tell(n):
+        pl.semaphore_signal(level.at[0, n], inc=1, device_id={"row": right, "col": c}, device_id_type=MESH)
+        pl.semaphore_signal(level.at[1, n], inc=1, device_id={"row": left, "col": c}, device_id_type=MESH)
+
+    def hear(n):
+        pl.semaphore_wait(level.at[0, n], 1)
+        pl.semaphore_wait(level.at[1, n], 1)
+
+    pl.semaphore_wait(barrier, 3)
+    tell(2)
 
     def remote(src, dst, ssem, rsem, zz, cc):
         return pltpu.make_async_remote_copy(
@@ -85,15 +99,54 @@
         lax.fori_loop(0, nz - 1, one, 0)
         remote(src_at(z, other), dst, ssem, rsem, z, other).start()
 
+    def scatter_near(src_at, dst, ssem, rsem):
+        def put(zz):
+            for cc in range(nc):
+                to = lax.rem(c + cc, nc)
+                remote(src_at(zz, to), dst, ssem, rsem, zz, to).start()
+
+        def both(d):
+            put(lax.rem(z + d, nz))
+            put(lax.rem(z + nz - d, nz))
+
+        remote(src_at(z, other), dst, ssem, rsem, z, other).start()
+        known = rows // 2
+        for d in range(1, known + 1):
+            both(d)
+
+        def one(d, carry):
+            hear(d + 1)
+            tell(d + 2)
+            both(d)
+            return carry
+
+        lax.fori_loop(known + 1, half, one, 0)
+        hear(half + 1)
+        put(lax.rem(z + half, nz))
+
     def landed(buf, ssem, rsem):
         every = buf.at[pl.ds(0, devs - 1)]
         return remote(every, every, ssem, rsem, z, other)
 
-    for u in range(2):
+    for load in loads[:4]:
+        load.wait()
+    pos = lax.broadcasted_iota(jnp.int32, rm_ref.shape, 1)
+    alive = jnp.where(((rm_ref[...] == 1) | (pos == 0)) & (pos < crop_ref[0]), 1.0, 0.0).astype(F32)
+    km_ref[...] = jnp.where(alive > 0.0, 0.0, -1000000000.0).astype(F32)
+    spot = lax.broadcasted_iota(jnp.int32, (rows, nc * cols), 1)
+    want = lax.broadcasted_iota(jnp.int32, (rows, nc * cols), 0) + z * rows
+    row_alive = jnp.sum(jnp.where(spot == want, alive, 0.0), axis=1, keepdims=True)
+    col_alive = alive[:, :cols]
+    for cc in range(1, nc):
+        col_alive = jnp.where(c == cc, alive[:, cc * cols:(cc + 1) * cols], col_alive)
+    pm_ref[...] = row_alive * col_alive
+
+    def by_channel(u):
         for q in range(4):
             wt[u, q * ch:(q + 1) * ch, :] = jnp.transpose(
                 mp_ref[u, :, q * ch:(q + 1) * ch].astype(F32)).astype(BF16)
-        mgt[u] = jnp.transpose(jnp.broadcast_to(mg_ref[u:u + 1, :], (ch, ch)))
+
+    by_channel(0)
 
     def project(u, r):
         sl = pl.ds(pl.multiple_of(r * cols, cols), cols)
@@ -106,6 +159,12 @@
         right = mask * jax.nn.sigmoid(pt[3 * ch:]) * pt[2 * ch:3 * ch]
         fl[pl.ds(r, ch, stride=rows), :] = left
         fr[pl.ds(r, ch, stride=rows), :] = right
+        if u == 0:
+            @pl.when(lax.rem(r, 2) == 1)
+            def _():
+                n = 2 + r // 2
+                hear(n)
+                tell(n + 1)
 
     def send_lr(u, k):
         pair = jnp.concatenate(
@@ -117,7 +176,8 @@
         )
         s_lr[k] = pair.astype(BF16)
         r_lr[u, k, c * nz + z] = s_lr[k, me]
-        scatter(
+        go = scatter_near if u == 0 and k == 0 else scatter
+        go(
             lambda zz, cc: s_lr.at[k, zz * nc + cc], r_lr.at[u, k, c * nz + z],
             sem_lr_s.at[k], sem_lr_r.at[u, k])
 
@@ -162,16 +222,18 @@
 
     for u in range(2):
         rows_loop(functools.partial(project, u))
-        if u == 0:
-            pl.semaphore_wait(barrier, devs - 1)
         for k in range(per):
             send_lr(u, k)
         gate_row(u)
         if u == 0:
+            for load in loads[4:]:
+                load.wait()
+            by_channel(1)
+            for w in range(2):
+                mgt[w] = jnp.transpose(jnp.broadcast_to(mg_ref[w:w + 1, :], (ch, ch)))
             for q in range(4):
                 apt[q * ch:(q + 1) * ch, :] = jnp.transpose(
                     ap_ref[:, q * ch:(q + 1) * ch].astype(F32)).astype(BF16)
-            abt[...] = jnp.transpose(ab_ref[...].astype(F32)).astype(BF16)
         for k in range(per):
             product(u, k)
         for k in range(per):
@@ -185,28 +247,30 @@
         sl = pl.ds(pl.multiple_of(r * cols, cols), cols)
         normed = norm_lanes(zb[sl, :].astype(F32), ag_ref[...]).astype(BF16)
         nall[c, sl, :] = normed
-        fb[pl.ds(r, abt.shape[0], stride=rows), :] = dot(abt[...], normed, NT)
+        fb[pl.ds(r, HEADS, stride=rows), :] = dot(ab_ref[...], normed, NT)
 
     rows_loop(normed_row)
     hr = HEADS * rows
     s_b[...] = fb[:hr, :].astype(BF16)
-    mine = lax.rem(z, half)
     to = z // half
-
-    def spread(step, carry):
-        zz = far_first(step)
-        remote(s_b, r_b.at[c * half + mine], sem_b.at[0], sem_b.at[1], zz, to).start()
-        return carry
-
-    lax.fori_loop(0, nz - 1, spread, 0)
+    many = nc * half // stride
+    res = lax.rem(z, stride)
+    slot = res * many + c * (half // stride) + lax.rem(z, half) // stride
+    hops = nz // stride
+
+    def bias_wait(count, i):
+        return remote(r_b.at[pl.ds(0, count)], r_b.at[pl.ds(0, count)], sem_b.at[0, i], sem_b.at[1, i], z, other)
+
+    for t in sorted(range(1, hops), key=lambda t: -min(t, hops - t)):
+        remote(s_b, r_b.at[slot], sem_b.at[0, 0], sem_b.at[1, 0], lax.rem(z + stride * t, nz), to).start()
 
     @pl.when(to == c)
     def _():
-        r_b[c * half + mine] = s_b[...]
+        r_b[slot] = s_b[...]
 
     @pl.when(to != c)
     def _():
-        remote(s_b, r_b.at[c * half + mine], sem_b.at[0], sem_b.at[1], z, other).start()
+        remote(s_b, r_b.at[slot], sem_b.at[0, 0], sem_b.at[1, 0], z, other).start()
 
     swap = remote(nall.at[c], nall.at[c], sem_n.at[0], sem_n.at[1], z, other)
     swap.start()
@@ -231,23 +295,32 @@
             wide.append(jnp.concatenate(parts, axis=0))
         sc[r] = dot(keys, jnp.concatenate(wide, axis=1), NN)
 
-    rows_loop(scores_row)
-
-    def bias_wait(count):
-        return remote(r_b.at[pl.ds(0, count)], r_b.at[pl.ds(0, count)], sem_b.at[0], sem_b.at[1], z, other)
-
     @pl.when(to == c)
     def _():
-        bias_wait(nz - 1).wait()
+        bias_wait(many - 1, 0).wait_recv()
+        bias_wait(hops - 1, 0).wait_send()
 
     @pl.when(to != c)
     def _():
-        bias_wait(nz).wait()
+        bias_wait(many, 0).wait_recv()
+        bias_wait(hops, 0).wait_send()
+
+    group = r_b.at[pl.ds(res * many, many)]
+    near = [lax.rem(z + nz + o, nz) for o in (2, 1, -1)]
+    for zz in near:
+        remote(group, group, sem_b.at[0, 1], sem_b.at[1, 1], zz, c).start()
+
+    rows_loop(scores_row)
+    bias_wait(len(near) * many, 1).wait()
 
     for kc in range(nc):
-        part = r_b[kc * half:(kc + 1) * half].astype(F32)
+        lots = half // stride
+        part = [
+            r_b[q * many + kc * lots:q * many + (kc + 1) * lots].astype(F32) for q in range(stride)
+        ]
         for h in range(HEADS):
-            tile = part[:, h * rows:(h + 1) * rows].reshape(half * rows, cols) + km_ref[kc:kc + 1, :]
+            tile = jnp.stack([p[:, h * rows:(h + 1) * rows] for p in part], axis=1).reshape(half * rows, cols)
+            tile = tile + km_ref[:, kc * cols:(kc + 1) * cols]
             bt[kc * cols:(kc + 1) * cols, h * cols:(h + 1) * cols] = jnp.transpose(tile)
 
     hd = ch // HEADS
@@ -279,25 +352,30 @@
         rows, cols, ch = pair_rep.shape
         per = ch // devs
         half = nz // 2
-        z, c = lax.axis_index("row"), lax.axis_index("col")
-        positions = jnp.arange(residue_mask.shape[0], dtype=jnp.int32)
-        alive = (((residue_mask == 1) | (positions == 0)) & (positions < crop_length[0])).astype(F32)
-        row_alive = lax.dynamic_slice_in_dim(alive, z * rows, rows, 0)
-        col_alive = lax.dynamic_slice_in_dim(alive, c * cols, cols, 0)
-        pair_mask = row_alive[:, None] * col_alive[None, :]
-        key_mask = jnp.where(alive > 0, 0.0, -1000000000.0).astype(F32).reshape(nc, cols)
         area = rows * cols
         vmem = pltpu.VMEM
         out = pl.pallas_call(
-            functools.partial(kernel, nz, nc, rows),
+            functools.partial(kernel, nz, nc, rows, 4),
             out_shape=jax.ShapeDtypeStruct((area, ch), BF16),
-            in_specs=[pl.BlockSpec(memory_space=vmem)] * 11,
+            in_specs=[pl.BlockSpec(memory_space=pltpu.SMEM)] + [pl.BlockSpec(memory_space=pl.ANY)] * 10,
             out_specs=pl.BlockSpec(memory_space=vmem),
             scratch_shapes=[
+                vmem((1, nc * cols), jnp.int32),
+                vmem((area, ch), BF16),
+                vmem(norm_gain.shape, F32),
+                vmem(mult_proj.shape, BF16),
+                vmem(mixed_gain.shape, F32),
+                vmem(mult_out.shape, BF16),
+                vmem((1, ch), F32),
+                vmem(att_proj.shape, BF16),
+                vmem((HEADS, ch), BF16),
+                vmem(att_out.shape, BF16),
+                pltpu.SemaphoreType.DMA((10,)),
+                vmem((rows, cols), F32),
+                vmem((1, nc * cols), F32),
                 vmem((2, 4 * ch, ch), BF16),
                 vmem((2, ch, ch), F32),
                 vmem((4 * ch, ch), BF16),
-                vmem((HEADS, ch), BF16),
                 vmem((area, ch), BF16),
                 vmem((area, ch), F32),
                 vmem((area, ch), BF16),
@@ -315,20 +393,21 @@
                 vmem((rows, nc * cols, HEADS * cols), F32),
                 vmem((rows, ch, nc * cols), BF16),
                 vmem((rows, ch, cols), F32),
+                pltpu.SemaphoreType.REGULAR((2, half + 2)),
                 pltpu.SemaphoreType.DMA((per,)),
                 pltpu.SemaphoreType.DMA((2, per)),
                 pltpu.SemaphoreType.DMA((per,)),
                 pltpu.SemaphoreType.DMA((2, per)),
                 pltpu.SemaphoreType.DMA((2,)),
-                pltpu.SemaphoreType.DMA((2,)),
+                pltpu.SemaphoreType.DMA((2, 2)),
             ],
             compiler_params=pltpu.CompilerParams(
-                collective_id=1, has_side_effects=True, vmem_limit_bytes=48 * 1024 * 1024
+                collective_id=1, has_side_effects=True, vmem_limit_bytes=62 * 1024 * 1024
             ),
             name="triangle",
         )(
-            pair_rep.reshape(area, ch), pair_mask, key_mask, norm_gain, mult_proj, mixed_gain, mult_out,
-            att_gain.reshape(1, ch), att_proj, att_bias, att_out,
+            crop_length, residue_mask.reshape(1, nc * cols), pair_rep.reshape(area, ch), norm_gain, mult_proj,
+            mixed_gain, mult_out, att_gain.reshape(1, ch), att_proj, att_bias.T, att_out,
         )
         return out.reshape(rows, cols, ch)
 

time: 224 us -> 209 us (0.933)
  Pallas kernels: 216 us -> 206 us
  local copies, waits for them, and re-layouts: 5.3 us -> 1.67 us
    pallas_call x1, Pallas kernels: 216 us -> 206 us  [local(): pl.pallas_call(functools.partial(kernel, nz, nc, rows, 4), out_shape=jax....]
    unnamed x18 -> x1, local copies, waits for them, and re-layouts: 5.15 us -> 1.67 us
where the time goes in v2:
time: 209 us
  Pallas kernels  206 us (99%)
    pallas_call x1, Pallas kernels, local(): pl.pallas_call(functools.partial(kernel, nz, nc, rows, 4), out_shape=jax....  206 us

profile of v2, /device:TPU:46, one launch (start us, length us, event | category | flops | bytes accessed | tf_op | source)
XLA Modules:
  0.0 208.6 jit_solution(14270017368781853706)
XLA Ops:
  0.7 206.3 %triangle.1 = bf16[1024,128]{1,0:T(8,128)(2,1)} custom-call(s32[1]{0:T(128)S(6)} %copy.13.crop_ref, s32[1,256]{1,0:T(1,128)} %bitcast.7, bf16[1024,128]{1,0:T(8,128)(2,1)} %bitcast.6, f32[2,128]{1,0:T(2,128)} %ng_hbm.1, bf16[2,128,640]{2,1,0:T(8,128)(2,1)} %mp_hbm.1, f32[2,128]{1,0:T(2,128)} %mg_hbm.1, bf16[2,128,128]{2,1,0:T(8,128)(2,1)} %mo_hbm.1, ...), custom_call_target="tpu_custom_call" | custom-call | tf_op jit(solution)/shard_map/triangle/pallas_call | solution.py:357
  207.0 1.7 copy.14

commit v3 on v2

--- a/solution.py
+++ b/solution.py
@@ -39,8 +39,8 @@
     nz, nc, rows, stride, crop_ref, rm_hbm, x_hbm, ng_hbm, mp_hbm, mg_hbm, mo_hbm, ag_hbm, ap_hbm, ab_hbm, ao_hbm,
     out_ref,
     rm_ref, x_ref, ng_ref, mp_ref, mg_ref, mo_ref, ag_ref, ap_ref, ab_ref, ao_ref, sem_in,
-    pm_ref, km_ref, wt, mgt, apt, nrm, gate, zb, fl, fr, s_lr, r_lr, s_p, r_p, nall, fb, s_b, r_b, bt, sc, vt, sg,
-    level, sem_lr_s, sem_lr_r, sem_p_s, sem_p_r, sem_n, sem_b,
+    pm_ref, km_ref, wt, mgt, apt, nrm, gate, zb, fl, fr, fp, s_lr, r_lr, s_l2, r_l2, s_p, r_p, s_q, r_q, nall, fb, s_b, r_b, bt, sc, vt, sg,
+    level, sem_lr, sem_l2, sem_p, sem_q, sem_n, sem_bf, sem_b,
 ):
     z = lax.axis_index("row")
     c = lax.axis_index("col")
@@ -56,7 +56,7 @@
     barrier = pltpu.get_barrier_semaphore()
 
     left, right = lax.rem(z + nz - 1, nz), lax.rem(z + 1, nz)
-    for zz, cc in ((left, c), (right, c), (z, other)):
+    for zz, cc in ((left, c), (right, c), (left, other), (right, other), (z, other)):
         pl.semaphore_signal(barrier, inc=1, device_id={"row": zz, "col": cc}, device_id_type=MESH)
     loads = []
     for i, (src, dst) in enumerate((
@@ -67,15 +67,16 @@
         loads[-1].start()
 
     def tell(n):
-        pl.semaphore_signal(level.at[0, n], inc=1, device_id={"row": right, "col": c}, device_id_type=MESH)
-        pl.semaphore_signal(level.at[1, n], inc=1, device_id={"row": left, "col": c}, device_id_type=MESH)
+        up, down = lax.rem(z + 2 ** n, nz), lax.rem(z + nz - 2 ** n, nz)
+        pl.semaphore_signal(level.at[0, n], inc=1, device_id={"row": up, "col": c}, device_id_type=MESH)
+        pl.semaphore_signal(level.at[1, n], inc=1, device_id={"row": down, "col": c}, device_id_type=MESH)
 
     def hear(n):
-        pl.semaphore_wait(level.at[0, n], 1)
-        pl.semaphore_wait(level.at[1, n], 1)
-
-    pl.semaphore_wait(barrier, 3)
-    tell(2)
+        pl.semaphore_wait(level.at[0, n - 1], 1)
+        pl.semaphore_wait(level.at[1, n - 1], 1)
+
+    pl.semaphore_wait(barrier, 5)
+    tell(0)
 
     def remote(src, dst, ssem, rsem, zz, cc):
         return pltpu.make_async_remote_copy(
@@ -99,30 +100,24 @@
         lax.fori_loop(0, nz - 1, one, 0)
         remote(src_at(z, other), dst, ssem, rsem, z, other).start()
 
-    def scatter_near(src_at, dst, ssem, rsem):
+    def ring(src_at, dst, ssem, rsem, near, far):
         def put(zz):
             for cc in range(nc):
                 to = lax.rem(c + cc, nc)
                 remote(src_at(zz, to), dst, ssem, rsem, zz, to).start()
 
-        def both(d):
+        def both(i, carry):
+            d = far - i
             put(lax.rem(z + d, nz))
             put(lax.rem(z + nz - d, nz))
-
-        remote(src_at(z, other), dst, ssem, rsem, z, other).start()
-        known = rows // 2
-        for d in range(1, known + 1):
-            both(d)
-
-        def one(d, carry):
-            hear(d + 1)
-            tell(d + 2)
-            both(d)
             return carry
 
-        lax.fori_loop(known + 1, half, one, 0)
-        hear(half + 1)
-        put(lax.rem(z + half, nz))
+        if near == 1:
+            remote(src_at(z, other), dst, ssem, rsem, z, other).start()
+        if far == half:
+            put(lax.rem(z + half, nz))
+            far -= 1
+        lax.fori_loop(0, far + 1 - near, both, 0)
 
     def landed(buf, ssem, rsem):
         every = buf.at[pl.ds(0, devs - 1)]
@@ -148,7 +143,9 @@
 
     by_channel(0)
 
-    def project(u, r):
+    hr = rows // 2
+
+    def project(u, r, hf=0):
         sl = pl.ds(pl.multiple_of(r * cols, cols), cols)
         src = x_ref if u == 0 else zb
         normed = norm_lanes(src[sl, :].astype(F32), ng_ref[u:u + 1, :]).astype(BF16)
@@ -157,16 +154,17 @@
         mask = pm_ref[pl.ds(r, 1), :]
         left = mask * jax.nn.sigmoid(pt[ch:2 * ch]) * pt[:ch]
         right = mask * jax.nn.sigmoid(pt[3 * ch:]) * pt[2 * ch:3 * ch]
-        fl[pl.ds(r, ch, stride=rows), :] = left
-        fr[pl.ds(r, ch, stride=rows), :] = right
         if u == 0:
-            @pl.when(lax.rem(r, 2) == 1)
-            def _():
-                n = 2 + r // 2
-                hear(n)
-                tell(n + 1)
-
-    def send_lr(u, k):
+            fl[pl.ds(r, ch, stride=rows), :] = left
+            fr[pl.ds(r, ch, stride=rows), :] = right
+        elif hf == 0:
+            fl[pl.ds(r, ch, stride=rows), :] = left
+            fl[pl.ds(r + hr, ch, stride=rows), :] = right
+        else:
+            fr[pl.ds(r, ch, stride=rows), :] = left
+            fr[pl.ds(r - hr, ch, stride=rows), :] = right
+
+    def pack(k):
         pair = jnp.concatenate(
             [
                 fl[k * block:(k + 1) * block, :].reshape(devs, rows, cols),
@@ -175,73 +173,125 @@
             axis=1,
         )
         s_lr[k] = pair.astype(BF16)
-        r_lr[u, k, c * nz + z] = s_lr[k, me]
-        go = scatter_near if u == 0 and k == 0 else scatter
-        go(
-            lambda zz, cc: s_lr.at[k, zz * nc + cc], r_lr.at[u, k, c * nz + z],
-            sem_lr_s.at[k], sem_lr_r.at[u, k])
-
-    def gate_row(u):
-        def one(r, carry):
-            sl = pl.ds(pl.multiple_of(r * cols, cols), cols)
-            gate[sl, :] = jax.nn.sigmoid(dot(nrm[sl, :], mp_ref[u, :, 4 * ch:], NN))
-            return carry
-
-        lax.fori_loop(0, rows, one, 0)
+        r_lr[k, c * nz + z] = s_lr[k, me]
+
+    def send_first(k, near, far):
+        ring(lambda zz, cc: s_lr.at[k, zz * nc + cc], r_lr.at[k, c * nz + z], sem_lr.at[0, k], sem_lr.at[1, k], near, far)
+
+    def send_second(hf, k):
+        src = fl if hf == 0 else fr
+        s_l2[hf, k] = src[k * block:(k + 1) * block, :].reshape(devs, rows, cols).astype(BF16)
+        r_l2[hf, k, c * nz + z] = s_l2[hf, k, me]
+        scatter(
+            lambda zz, cc: s_l2.at[hf, k, zz * nc + cc], r_l2.at[hf, k, c * nz + z],
+            sem_l2.at[0, hf, k], sem_l2.at[1, hf, k])
+
+    def gate_row(u, r):
+        sl = pl.ds(pl.multiple_of(r * cols, cols), cols)
+        gate[sl, :] = jax.nn.sigmoid(dot(nrm[sl, :], mp_ref[u, :, 4 * ch:], NN))
 
     def product(u, k):
-        wait = landed(r_lr.at[u, k], sem_lr_s.at[k], sem_lr_r.at[u, k])
-        wait.wait_recv()
         lefts, rights = [], []
-        for cc in range(nc):
-            part = r_lr[u, k, cc * nz:(cc + 1) * nz].astype(F32)
-            lefts.append(part[:, :rows].reshape(nz * rows, cols).astype(BF16))
-            rights.append(part[:, rows:].reshape(nz * rows, cols).astype(BF16))
+        if u == 0:
+            landed(r_lr.at[k], sem_lr.at[0, k], sem_lr.at[1, k]).wait_recv()
+            for cc in range(nc):
+                part = r_lr[k, cc * nz:(cc + 1) * nz].astype(F32)
+                lefts.append(part[:, :rows].reshape(nz * rows, cols).astype(BF16))
+                rights.append(part[:, rows:].reshape(nz * rows, cols).astype(BF16))
+        else:
+            for hf in range(2):
+                landed(r_l2.at[hf, k], sem_l2.at[0, hf, k], sem_l2.at[1, hf, k]).wait_recv()
+            low = lax.broadcasted_iota(jnp.int32, (nz, rows, cols), 1) < hr
+            for cc in range(nc):
+                first = r_l2[0, k, cc * nz:(cc + 1) * nz].astype(F32)
+                last = r_l2[1, k, cc * nz:(cc + 1) * nz].astype(F32)
+                lefts.append(jnp.where(low, first, last).reshape(nz * rows, cols).astype(BF16))
+                turned = pltpu.roll(jnp.where(low, last, first), hr, 1)
+                rights.append(turned.reshape(nz * rows, cols).astype(BF16))
         left = jnp.concatenate(lefts, axis=1)
         right = jnp.concatenate(rights, axis=1)
         prod = dot(left, right, NT if u == 0 else TN)
-        for cc in range(nc):
-            s_p[k, cc] = prod[:, cc * cols:(cc + 1) * cols].reshape(nz, rows, cols).astype(BF16)
-        r_p[u, k, me] = s_p[k, c, z]
-        scatter(lambda zz, cc: s_p.at[k, cc, zz], r_p.at[u, k, me], sem_p_s.at[k], sem_p_r.at[u, k])
-        wait.wait_send()
+        tiles = [prod[:, cc * cols:(cc + 1) * cols].reshape(nz, rows, cols) for cc in range(nc)]
+        if k == 0:
+            for cc in range(nc):
+                s_p[u, cc] = tiles[cc].astype(BF16)
+            r_p[u, me] = s_p[u, c, z]
+            scatter(lambda zz, cc: s_p.at[u, cc, zz], r_p.at[u, me], sem_p.at[0, u], sem_p.at[1, u])
+            return
+        for hf in range(2):
+            for cc in range(nc):
+                s_q[u, hf, cc] = tiles[cc][:, hf * hr:(hf + 1) * hr].astype(BF16)
+            r_q[u, hf, me] = s_q[u, hf, c, z]
+            scatter(
+                lambda zz, cc: s_q.at[u, hf, cc, zz], r_q.at[u, hf, me], sem_q.at[0, u, hf], sem_q.at[1, u, hf])
+
+    def returned(u, hf):
+        if hf == 0:
+            landed(r_p.at[u], sem_p.at[0, u], sem_p.at[1, u]).wait_recv()
+            fp[:block, :] = r_p[u].astype(F32).reshape(block, cols)
+        landed(r_q.at[u, hf], sem_q.at[0, u, hf], sem_q.at[1, u, hf]).wait_recv()
+        view = fp.reshape(ch, rows, cols)
+        view[devs:, hf * hr:(hf + 1) * hr, :] = r_q[u, hf].astype(F32)
 
     def updated(u, r):
         sl = pl.ds(pl.multiple_of(r * cols, cols), cols)
-        mixed = norm_sublanes(fl[pl.ds(r, ch, stride=rows), :], mgt[u]).astype(BF16)
+        mixed = norm_sublanes(fp[pl.ds(r, ch, stride=rows), :], mgt[u]).astype(BF16)
         upd = dot(mixed, mo_ref[u], TN)
         src = x_ref if u == 0 else zb
         zb[sl, :] = (src[sl, :].astype(F32) + gate[sl, :] * upd).astype(BF16)
 
-    def rows_loop(f):
-        def one(r, carry):
-            f(r)
+    def rows_loop(f, lo=0, hi=rows, step=2):
+        def some(i, carry):
+            for t in range(step):
+                f(lo + i * step + t)
             return carry
 
-        lax.fori_loop(0, rows, one, 0)
-
-    for u in range(2):
-        rows_loop(functools.partial(project, u))
+        lax.fori_loop(0, (hi - lo) // step, some, 0)
+
+    def first_row(r):
+        project(0, r)
+
+    rows_loop(first_row, 0, hr)
+    hear(1)
+    tell(1)
+    rows_loop(first_row, hr, rows)
+    pack(0)
+    hear(2)
+    tell(2)
+    send_first(0, 1, 4)
+    pack(1)
+    send_first(1, 1, 4)
+    for load in loads[4:]:
+        load.wait()
+    by_channel(1)
+    hear(3)
+    tell(3)
+    send_first(0, 5, 8)
+    send_first(1, 5, 8)
+    rows_loop(functools.partial(gate_row, 0))
+    hear(4)
+    send_first(0, 9, half)
+    send_first(1, 9, half)
+    for w in range(2):
+        mgt[w] = jnp.transpose(jnp.broadcast_to(mg_ref[w:w + 1, :], (ch, ch)))
+    for q in range(4):
+        apt[q * ch:(q + 1) * ch, :] = jnp.transpose(
+            ap_ref[:, q * ch:(q + 1) * ch].astype(F32)).astype(BF16)
+    for k in range(per):
+        product(0, k)
+    for hf in range(2):
+        returned(0, hf)
+
+        def both_steps(r, hf=hf):
+            updated(0, r)
+            project(1, r, hf)
+
+        rows_loop(both_steps, hf * hr, (hf + 1) * hr)
         for k in range(per):
-            send_lr(u, k)
-        gate_row(u)
-        if u == 0:
-            for load in loads[4:]:
-                load.wait()
-            by_channel(1)
-            for w in range(2):
-                mgt[w] = jnp.transpose(jnp.broadcast_to(mg_ref[w:w + 1, :], (ch, ch)))
-            for q in range(4):
-                apt[q * ch:(q + 1) * ch, :] = jnp.transpose(
-                    ap_ref[:, q * ch:(q + 1) * ch].astype(F32)).astype(BF16)
-        for k in range(per):
-            product(u, k)
-        for k in range(per):
-            wait = landed(r_p.at[u, k], sem_p_s.at[k], sem_p_r.at[u, k])
-            wait.wait_recv()
-            fl[k * block:(k + 1) * block, :] = r_p[u, k].astype(F32).reshape(block, cols)
-            wait.wait_send()
-        rows_loop(functools.partial(updated, u))
+            send_second(hf, k)
+    rows_loop(functools.partial(gate_row, 1))
+    for k in range(per):
+        product(1, k)
 
     def normed_row(r):
         sl = pl.ds(pl.multiple_of(r * cols, cols), cols)
@@ -249,20 +299,28 @@
         nall[c, sl, :] = normed
         fb[pl.ds(r, HEADS, stride=rows), :] = dot(ab_ref[...], normed, NT)
 
-    rows_loop(normed_row)
-    hr = HEADS * rows
-    s_b[...] = fb[:hr, :].astype(BF16)
+    for hf in range(2):
+        returned(1, hf)
+
+        def last_steps(r):
+            updated(1, r)
+            normed_row(r)
+
+        rows_loop(last_steps, hf * hr, (hf + 1) * hr)
+    s_b[...] = fb[...].astype(BF16)
     to = z // half
-    many = nc * half // stride
+    lots = half // stride
+    many = nc * lots
     res = lax.rem(z, stride)
-    slot = res * many + c * (half // stride) + lax.rem(z, half) // stride
+    turn = lax.rem(z, half) // stride
+    slot = res * many + turn * nc + c
     hops = nz // stride
 
-    def bias_wait(count, i):
-        return remote(r_b.at[pl.ds(0, count)], r_b.at[pl.ds(0, count)], sem_b.at[0, i], sem_b.at[1, i], z, other)
+    def bias_wait(count, ssem, rsem):
+        return remote(r_b.at[pl.ds(0, count)], r_b.at[pl.ds(0, count)], ssem, rsem, z, other)
 
     for t in sorted(range(1, hops), key=lambda t: -min(t, hops - t)):
-        remote(s_b, r_b.at[slot], sem_b.at[0, 0], sem_b.at[1, 0], lax.rem(z + stride * t, nz), to).start()
+        remote(s_b, r_b.at[slot], sem_b.at[0], sem_bf.at[turn], lax.rem(z + stride * t, nz), to).start()
 
     @pl.when(to == c)
     def _():
@@ -270,11 +328,10 @@
 
     @pl.when(to != c)
     def _():
-        remote(s_b, r_b.at[slot], sem_b.at[0, 0], sem_b.at[1, 0], z, other).start()
+        remote(s_b, r_b.at[slot], sem_b.at[0], sem_bf.at[turn], z, other).start()
 
     swap = remote(nall.at[c], nall.at[c], sem_n.at[0], sem_n.at[1], z, other)
     swap.start()
-    swap.wait()
 
     def scores_row(r):
         sl = pl.ds(pl.multiple_of(r * cols, cols), cols)
@@ -295,28 +352,26 @@
             wide.append(jnp.concatenate(parts, axis=0))
         sc[r] = dot(keys, jnp.concatenate(wide, axis=1), NN)
 
-    @pl.when(to == c)
-    def _():
-        bias_wait(many - 1, 0).wait_recv()
-        bias_wait(hops - 1, 0).wait_send()
-
-    @pl.when(to != c)
-    def _():
-        bias_wait(many, 0).wait_recv()
-        bias_wait(hops, 0).wait_send()
-
-    group = r_b.at[pl.ds(res * many, many)]
+    swap.wait()
+    rows_loop(scores_row)
+
     near = [lax.rem(z + nz + o, nz) for o in (2, 1, -1)]
-    for zz in near:
-        remote(group, group, sem_b.at[0, 1], sem_b.at[1, 1], zz, c).start()
-
-    rows_loop(scores_row)
-    bias_wait(len(near) * many, 1).wait()
+    for t in sorted(range(hops), key=lambda t: min(t, hops - t)):
+        zz = lax.rem(z + stride * t, nz)
+        src_turn = lax.rem(zz, half) // stride
+
+        @pl.when(zz // half == c)
+        def _(t=t, src_turn=src_turn):
+            bias_wait(nc - 1 if t == 0 else nc, sem_b.at[0], sem_bf.at[src_turn]).wait_recv()
+            group = r_b.at[pl.ds(res * many + src_turn * nc, nc)]
+            for beside in near:
+                remote(group, group, sem_b.at[1], sem_b.at[2], beside, c).start()
+
+    bias_wait(len(near) * many, sem_b.at[1], sem_b.at[2]).wait()
 
     for kc in range(nc):
-        lots = half // stride
         part = [
-            r_b[q * many + kc * lots:q * many + (kc + 1) * lots].astype(F32) for q in range(stride)
+            jnp.stack([r_b[q * many + m * nc + kc] for m in range(lots)]).astype(F32) for q in range(stride)
         ]
         for h in range(HEADS):
             tile = jnp.stack([p[:, h * rows:(h + 1) * rows] for p in part], axis=1).reshape(half * rows, cols)
@@ -341,6 +396,21 @@
         out_ref[sl, :] = (zb[sl, :].astype(F32) + dot(gated, ao_ref[...], TN)).astype(BF16)
 
     rows_loop(attend_row)
+
+    for k in range(per):
+        landed(r_lr.at[k], sem_lr.at[0, k], sem_lr.at[1, k]).wait_send()
+        landed(r_p.at[k], sem_p.at[0, k], sem_p.at[1, k]).wait_send()
+        for hf in range(2):
+            landed(r_l2.at[hf, k], sem_l2.at[0, hf, k], sem_l2.at[1, hf, k]).wait_send()
+            landed(r_q.at[k, hf], sem_q.at[0, k, hf], sem_q.at[1, k, hf]).wait_send()
+
+    @pl.when(to == c)
+    def _():
+        bias_wait(hops - 1, sem_b.at[0], sem_b.at[2]).wait_send()
+
+    @pl.when(to != c)
+    def _():
+        bias_wait(hops, sem_b.at[0], sem_b.at[2]).wait_send()
 
 
 def solution(mesh):
@@ -381,10 +451,15 @@
                 vmem((area, ch), BF16),
                 vmem((ch * rows, cols), F32),
                 vmem((ch * rows, cols), F32),
+                vmem((ch * rows, cols), F32),
                 vmem((per, devs, 2 * rows, cols), BF16),
-                vmem((2, per, devs, 2 * rows, cols), BF16),
-                vmem((per, nc, nz, rows, cols), BF16),
+                vmem((per, devs, 2 * rows, cols), BF16),
                 vmem((2, per, devs, rows, cols), BF16),
+                vmem((2, per, devs, rows, cols), BF16),
+                vmem((2, nc, nz, rows, cols), BF16),
+                vmem((2, devs, rows, cols), BF16),
+                vmem((2, 2, nc, nz, rows // 2, cols), BF16),
+                vmem((2, 2, devs, rows // 2, cols), BF16),
                 vmem((nc, area, ch), BF16),
                 vmem((HEADS * rows, cols), F32),
                 vmem((HEADS * rows, cols), BF16),
@@ -393,13 +468,14 @@
                 vmem((rows, nc * cols, HEADS * cols), F32),
                 vmem((rows, ch, nc * cols), BF16),
                 vmem((rows, ch, cols), F32),
-                pltpu.SemaphoreType.REGULAR((2, half + 2)),
-                pltpu.SemaphoreType.DMA((per,)),
+                pltpu.SemaphoreType.REGULAR((2, 4)),
                 pltpu.SemaphoreType.DMA((2, per)),
-                pltpu.SemaphoreType.DMA((per,)),
-                pltpu.SemaphoreType.DMA((2, per)),
+                pltpu.SemaphoreType.DMA((2, 2, per)),
+                pltpu.SemaphoreType.DMA((2, 2)),
+                pltpu.SemaphoreType.DMA((2, 2, 2)),
                 pltpu.SemaphoreType.DMA((2,)),
-                pltpu.SemaphoreType.DMA((2, 2)),
+                pltpu.SemaphoreType.DMA((half // 4,)),
+                pltpu.SemaphoreType.DMA((3,)),
             ],
             compiler_params=pltpu.CompilerParams(
                 collective_id=1, has_side_effects=True, vmem_limit_bytes=62 * 1024 * 1024

time: 209 us -> 199 us (0.952)
  Pallas kernels: 206 us -> 196 us
    pallas_call x1, Pallas kernels: 206 us -> 196 us  [local(): pl.pallas_call(functools.partial(kernel, nz, nc, rows, 4), out_shape=jax....]
where the time goes in v3:
time: 199 us; the launch traced here: 198 us
  Pallas kernels  196 us (98%)
    pallas_call x1, Pallas kernels, local(): pl.pallas_call(functools.partial(kernel, nz, nc, rows, 4), out_shape=jax....  196 us

profile of v3, /device:TPU:46, one launch (start us, length us, event | category | flops | bytes accessed | tf_op | source)
XLA Modules:
  0.0 197.9 jit_solution(17757844930095886814)
XLA Ops:
  0.7 195.5 %triangle.1 = bf16[1024,128]{1,0:T(8,128)(2,1)} custom-call(s32[1]{0:T(128)S(6)} %copy.13.crop_ref, s32[1,256]{1,0:T(1,128)} %bitcast.7, bf16[1024,128]{1,0:T(8,128)(2,1)} %bitcast.6, f32[2,128]{1,0:T(2,128)} %ng_hbm.1, bf16[2,128,640]{2,1,0:T(8,128)(2,1)} %mp_hbm.1, f32[2,128]{1,0:T(2,128)} %mg_hbm.1, bf16[2,128,128]{2,1,0:T(8,128)(2,1)} %mo_hbm.1, ...), custom_call_target="tpu_custom_call" | custom-call | tf_op jit(solution)/shard_map/triangle/pallas_call | solution.py:427
  196.2 1.7 copy.14

commit v4 on v3

--- a/solution.py
+++ b/solution.py
@@ -36,11 +36,11 @@
 
 
 def kernel(
-    nz, nc, rows, stride, crop_ref, rm_hbm, x_hbm, ng_hbm, mp_hbm, mg_hbm, mo_hbm, ag_hbm, ap_hbm, ab_hbm, ao_hbm,
-    out_ref,
+    nz, nc, rows, stride, reach, crop_ref, rm_hbm, x_hbm, ng_hbm, mp_hbm, mg_hbm, mo_hbm, ag_hbm, ap_hbm, ab_hbm, ao_hbm,
+    out_hbm,
     rm_ref, x_ref, ng_ref, mp_ref, mg_ref, mo_ref, ag_ref, ap_ref, ab_ref, ao_ref, sem_in,
-    pm_ref, km_ref, wt, mgt, apt, nrm, gate, zb, fl, fr, fp, s_lr, r_lr, s_l2, r_l2, s_p, r_p, s_q, r_q, nall, fb, s_b, r_b, bt, sc, vt, sg,
-    level, sem_lr, sem_l2, sem_p, sem_q, sem_n, sem_bf, sem_b,
+    pm_ref, km_ref, wt, mgt, apt, nrm, gate, zb, fl, fr, fp, s_lr, r_lr, s_l2, r_l2, s_p, r_p, s_q, r_q, nall, fb, s_b, r_b, bt, sc, vt, sg, ob,
+    level, sem_lr, sem_l2, sem_p, sem_q, sem_n, sem_bf, sem_bs, sem_b, sem_o,
 ):
     z = lax.axis_index("row")
     c = lax.axis_index("col")
@@ -48,6 +48,7 @@
     devs = nz * nc
     cols = pm_ref.shape[1]
     ch = x_ref.shape[1]
+    hd = ch // HEADS
     per = s_lr.shape[0]
     block = devs * rows
     half = nz // 2
@@ -55,9 +56,11 @@
 
     barrier = pltpu.get_barrier_semaphore()
 
-    left, right = lax.rem(z + nz - 1, nz), lax.rem(z + 1, nz)
-    for zz, cc in ((left, c), (right, c), (left, other), (right, other), (z, other)):
-        pl.semaphore_signal(barrier, inc=1, device_id={"row": zz, "col": cc}, device_id_type=MESH)
+    for d in range(1, reach + 1):
+        for zz in (lax.rem(z + d, nz), lax.rem(z + nz - d, nz)):
+            for cc in (c, other):
+                pl.semaphore_signal(barrier, inc=1, device_id={"row": zz, "col": cc}, device_id_type=MESH)
+    pl.semaphore_signal(barrier, inc=1, device_id={"row": z, "col": other}, device_id_type=MESH)
     loads = []
     for i, (src, dst) in enumerate((
         (x_hbm, x_ref), (ng_hbm, ng_ref), (mp_hbm, mp_ref), (rm_hbm, rm_ref), (mg_hbm, mg_ref), (mo_hbm, mo_ref),
@@ -66,17 +69,14 @@
         loads.append(pltpu.make_async_copy(src, dst, sem_in.at[i]))
         loads[-1].start()
 
-    def tell(n):
-        up, down = lax.rem(z + 2 ** n, nz), lax.rem(z + nz - 2 ** n, nz)
+    def tell(d, n):
+        up, down = lax.rem(z + d, nz), lax.rem(z + nz - d, nz)
         pl.semaphore_signal(level.at[0, n], inc=1, device_id={"row": up, "col": c}, device_id_type=MESH)
         pl.semaphore_signal(level.at[1, n], inc=1, device_id={"row": down, "col": c}, device_id_type=MESH)
 
     def hear(n):
-        pl.semaphore_wait(level.at[0, n - 1], 1)
-        pl.semaphore_wait(level.at[1, n - 1], 1)
-
-    pl.semaphore_wait(barrier, 5)
-    tell(0)
+        pl.semaphore_wait(level.at[0, n], 1)
+        pl.semaphore_wait(level.at[1, n], 1)
 
     def remote(src, dst, ssem, rsem, zz, cc):
         return pltpu.make_async_remote_copy(
@@ -84,40 +84,26 @@
             device_id={"row": zz, "col": cc}, device_id_type=MESH,
         )
 
-    def far_first(step):
-        d = half - (step + 1) // 2
-        off = jnp.where(lax.rem(step, 2) == 1, d, nz - d)
-        return lax.rem(z + off, nz)
-
-    def scatter(src_at, dst, ssem, rsem):
-        def one(step, carry):
-            zz = far_first(step)
-            for cc in range(nc):
-                to = lax.rem(c + cc, nc)
-                remote(src_at(zz, to), dst, ssem, rsem, zz, to).start()
-            return carry
-
-        lax.fori_loop(0, nz - 1, one, 0)
-        remote(src_at(z, other), dst, ssem, rsem, z, other).start()
-
     def ring(src_at, dst, ssem, rsem, near, far):
         def put(zz):
-            for cc in range(nc):
-                to = lax.rem(c + cc, nc)
-                remote(src_at(zz, to), dst, ssem, rsem, zz, to).start()
+            remote(src_at(zz, c), dst, ssem, rsem, zz, c).start()
+            remote(src_at(zz, other), dst, ssem, rsem, zz, other).start()
 
         def both(i, carry):
-            d = far - i
-            put(lax.rem(z + d, nz))
-            put(lax.rem(z + nz - d, nz))
+            up, down = z + far - i, z - far + i
+            put(jnp.where(up >= nz, up - nz, up))
+            put(jnp.where(down < 0, down + nz, down))
             return carry
 
-        if near == 1:
-            remote(src_at(z, other), dst, ssem, rsem, z, other).start()
         if far == half:
             put(lax.rem(z + half, nz))
             far -= 1
         lax.fori_loop(0, far + 1 - near, both, 0)
+        if near == 1:
+            remote(src_at(z, other), dst, ssem, rsem, z, other).start()
+
+    def scatter(src_at, dst, ssem, rsem):
+        ring(src_at, dst, ssem, rsem, 1, half)
 
     def landed(buf, ssem, rsem):
         every = buf.at[pl.ds(0, devs - 1)]
@@ -212,26 +198,27 @@
         right = jnp.concatenate(rights, axis=1)
         prod = dot(left, right, NT if u == 0 else TN)
         tiles = [prod[:, cc * cols:(cc + 1) * cols].reshape(nz, rows, cols) for cc in range(nc)]
-        if k == 0:
+        if u or k == 0:
+            n = u + k
             for cc in range(nc):
-                s_p[u, cc] = tiles[cc].astype(BF16)
-            r_p[u, me] = s_p[u, c, z]
-            scatter(lambda zz, cc: s_p.at[u, cc, zz], r_p.at[u, me], sem_p.at[0, u], sem_p.at[1, u])
+                s_p[n, cc] = tiles[cc].astype(BF16)
+            r_p[n, me] = s_p[n, c, z]
+            scatter(lambda zz, cc: s_p.at[n, cc, zz], r_p.at[n, me], sem_p.at[0, n], sem_p.at[1, n])
             return
         for hf in range(2):
             for cc in range(nc):
-                s_q[u, hf, cc] = tiles[cc][:, hf * hr:(hf + 1) * hr].astype(BF16)
-            r_q[u, hf, me] = s_q[u, hf, c, z]
-            scatter(
-                lambda zz, cc: s_q.at[u, hf, cc, zz], r_q.at[u, hf, me], sem_q.at[0, u, hf], sem_q.at[1, u, hf])
-
-    def returned(u, hf):
-        if hf == 0:
-            landed(r_p.at[u], sem_p.at[0, u], sem_p.at[1, u]).wait_recv()
-            fp[:block, :] = r_p[u].astype(F32).reshape(block, cols)
-        landed(r_q.at[u, hf], sem_q.at[0, u, hf], sem_q.at[1, u, hf]).wait_recv()
+                s_q[hf, cc] = tiles[cc][:, hf * hr:(hf + 1) * hr].astype(BF16)
+            r_q[hf, me] = s_q[hf, c, z]
+            scatter(lambda zz, cc: s_q.at[hf, cc, zz], r_q.at[hf, me], sem_q.at[0, hf], sem_q.at[1, hf])
+
+    def whole(n, k):
+        landed(r_p.at[n], sem_p.at[0, n], sem_p.at[1, n]).wait_recv()
+        fp[k * block:(k + 1) * block, :] = r_p[n].astype(F32).reshape(block, cols)
+
+    def part(hf):
+        landed(r_q.at[hf], sem_q.at[0, hf], sem_q.at[1, hf]).wait_recv()
         view = fp.reshape(ch, rows, cols)
-        view[devs:, hf * hr:(hf + 1) * hr, :] = r_q[u, hf].astype(F32)
+        view[devs:, hf * hr:(hf + 1) * hr, :] = r_q[hf].astype(F32)
 
     def updated(u, r):
         sl = pl.ds(pl.multiple_of(r * cols, cols), cols)
@@ -251,27 +238,24 @@
     def first_row(r):
         project(0, r)
 
-    rows_loop(first_row, 0, hr)
-    hear(1)
-    tell(1)
-    rows_loop(first_row, hr, rows)
+    rows_loop(first_row)
+    pl.semaphore_wait(barrier, (2 * reach) * nc + 1)
+    tell(reach, 0)
     pack(0)
-    hear(2)
-    tell(2)
-    send_first(0, 1, 4)
+    send_first(0, 1, reach)
     pack(1)
-    send_first(1, 1, 4)
+    send_first(1, 1, reach)
     for load in loads[4:]:
         load.wait()
     by_channel(1)
-    hear(3)
-    tell(3)
-    send_first(0, 5, 8)
-    send_first(1, 5, 8)
+    hear(0)
+    tell(2 * reach, 1)
+    send_first(0, reach + 1, 2 * reach)
+    send_first(1, reach + 1, 2 * reach)
     rows_loop(functools.partial(gate_row, 0))
-    hear(4)
-    send_first(0, 9, half)
-    send_first(1, 9, half)
+    hear(1)
+    send_first(0, 2 * reach + 1, half)
+    send_first(1, 2 * reach + 1, half)
     for w in range(2):
         mgt[w] = jnp.transpose(jnp.broadcast_to(mg_ref[w:w + 1, :], (ch, ch)))
     for q in range(4):
@@ -279,8 +263,9 @@
             ap_ref[:, q * ch:(q + 1) * ch].astype(F32)).astype(BF16)
     for k in range(per):
         product(0, k)
+    whole(0, 0)
     for hf in range(2):
-        returned(0, hf)
+        part(hf)
 
         def both_steps(r, hf=hf):
             updated(0, r)
@@ -299,14 +284,14 @@
         nall[c, sl, :] = normed
         fb[pl.ds(r, HEADS, stride=rows), :] = dot(ab_ref[...], normed, NT)
 
-    for hf in range(2):
-        returned(1, hf)
-
-        def last_steps(r):
-            updated(1, r)
-            normed_row(r)
-
-        rows_loop(last_steps, hf * hr, (hf + 1) * hr)
+    whole(1, 0)
+    whole(2, 1)
+
+    def last_steps(r):
+        updated(1, r)
+        normed_row(r)
+
+    rows_loop(last_steps, step=4)
     s_b[...] = fb[...].astype(BF16)
     to = z // half
     lots = half // stride
@@ -342,7 +327,6 @@
         keys = dot(full, ap_ref[:, ch:2 * ch], NN).astype(BF16)
         vt[r] = dot(apt[2 * ch:3 * ch], full, NT).astype(BF16)
         sg[r] = jax.nn.sigmoid(gt.astype(F32))
-        hd = ch // HEADS
         wide = []
         for h in range(HEADS):
             parts = [jnp.zeros((h * hd, cols), BF16)] if h else []
@@ -350,25 +334,32 @@
             if h < HEADS - 1:
                 parts.append(jnp.zeros(((HEADS - 1 - h) * hd, cols), BF16))
             wide.append(jnp.concatenate(parts, axis=0))
-        sc[r] = dot(keys, jnp.concatenate(wide, axis=1), NN)
+        sc[r] = dot(keys, jnp.concatenate(wide, axis=1), NN) * (1.0 / float(hd) ** 0.5)
 
     swap.wait()
     rows_loop(scores_row)
 
+    ahead = lax.rem(z + nz - c * half, nz)
+    rising = (ahead < half // 2) | (ahead >= nz - half // 2)
+    order = [jnp.where(rising, i, lots - 1 - i) for i in range(lots)]
     near = [lax.rem(z + nz + o, nz) for o in (2, 1, -1)]
-    for t in sorted(range(hops), key=lambda t: min(t, hops - t)):
-        zz = lax.rem(z + stride * t, nz)
-        src_turn = lax.rem(zz, half) // stride
-
-        @pl.when(zz // half == c)
-        def _(t=t, src_turn=src_turn):
-            bias_wait(nc - 1 if t == 0 else nc, sem_b.at[0], sem_bf.at[src_turn]).wait_recv()
-            group = r_b.at[pl.ds(res * many + src_turn * nc, nc)]
-            for beside in near:
-                remote(group, group, sem_b.at[1], sem_b.at[2], beside, c).start()
-
-    bias_wait(len(near) * many, sem_b.at[1], sem_b.at[2]).wait()
-
+    for m in order:
+        here = c * half + m * stride + res == z
+
+        @pl.when(here)
+        def _(m=m):
+            bias_wait(nc - 1, sem_b.at[0], sem_bf.at[m]).wait_recv()
+
+        @pl.when(jnp.logical_not(here))
+        def _(m=m):
+            bias_wait(nc, sem_b.at[0], sem_bf.at[m]).wait_recv()
+
+        group = r_b.at[pl.ds(res * many + m * nc, nc)]
+        for beside in near:
+            remote(group, group, sem_b.at[1], sem_bs.at[m], beside, c).start()
+
+    for m in order:
+        bias_wait(len(near) * nc, sem_b.at[1], sem_bs.at[m]).wait_recv()
     for kc in range(nc):
         part = [
             jnp.stack([r_b[q * many + m * nc + kc] for m in range(lots)]).astype(F32) for q in range(stride)
@@ -378,12 +369,9 @@
             tile = tile + km_ref[:, kc * cols:(kc + 1) * cols]
             bt[kc * cols:(kc + 1) * cols, h * cols:(h + 1) * cols] = jnp.transpose(tile)
 
-    hd = ch // HEADS
-    scale = 1.0 / float(hd) ** 0.5
-
     def attend_row(r):
         sl = pl.ds(pl.multiple_of(r * cols, cols), cols)
-        score = sc[r] * scale + bt[...]
+        score = sc[r] + bt[...]
         top = jnp.max(score, axis=0, keepdims=True)
         e = jnp.exp(score - top)
         inv = 1.0 / jnp.sum(e, axis=0, keepdims=True)
@@ -393,24 +381,39 @@
             lanes = slice(h * cols, (h + 1) * cols)
             parts.append(got[h * hd:(h + 1) * hd, lanes] * inv[:, lanes])
         gated = (sg[r] * jnp.concatenate(parts, axis=0)).astype(BF16)
-        out_ref[sl, :] = (zb[sl, :].astype(F32) + dot(gated, ao_ref[...], TN)).astype(BF16)
-
-    rows_loop(attend_row)
+        ob[r] = (zb[sl, :].astype(F32) + dot(gated, ao_ref[...], TN)).astype(BF16)
+
+    def leave(i):
+        some = pl.ds(i * 2, 2)
+        return pltpu.make_async_copy(ob.at[some], out_hbm.at[some], sem_o.at[i])
+
+    def two_rows(i, carry):
+        attend_row(2 * i)
+        attend_row(2 * i + 1)
+        leave(i).start()
+        return carry
+
+    lax.fori_loop(0, rows // 2, two_rows, 0)
 
     for k in range(per):
         landed(r_lr.at[k], sem_lr.at[0, k], sem_lr.at[1, k]).wait_send()
-        landed(r_p.at[k], sem_p.at[0, k], sem_p.at[1, k]).wait_send()
+        landed(r_q.at[k], sem_q.at[0, k], sem_q.at[1, k]).wait_send()
         for hf in range(2):
             landed(r_l2.at[hf, k], sem_l2.at[0, hf, k], sem_l2.at[1, hf, k]).wait_send()
-            landed(r_q.at[k, hf], sem_q.at[0, k, hf], sem_q.at[1, k, hf]).wait_send()
+    for n in range(3):
+        landed(r_p.at[n], sem_p.at[0, n], sem_p.at[1, n]).wait_send()
 
     @pl.when(to == c)
     def _():
-        bias_wait(hops - 1, sem_b.at[0], sem_b.at[2]).wait_send()
+        bias_wait(hops - 1, sem_b.at[0], sem_bf.at[0]).wait_send()
 
     @pl.when(to != c)
     def _():
-        bias_wait(hops, sem_b.at[0], sem_b.at[2]).wait_send()
+        bias_wait(hops, sem_b.at[0], sem_bf.at[0]).wait_send()
+
+    bias_wait(len(near) * many, sem_b.at[1], sem_bf.at[0]).wait_send()
+    for i in range(rows // 2):
+        leave(i).wait()
 
 
 def solution(mesh):
@@ -422,13 +425,15 @@
         rows, cols, ch = pair_rep.shape
         per = ch // devs
         half = nz // 2
+        stride = 4
+        lots = half // stride
         area = rows * cols
         vmem = pltpu.VMEM
         out = pl.pallas_call(
-            functools.partial(kernel, nz, nc, rows, 4),
-            out_shape=jax.ShapeDtypeStruct((area, ch), BF16),
+            functools.partial(kernel, nz, nc, rows, stride, 4),
+            out_shape=jax.ShapeDtypeStruct((rows, cols, ch), BF16),
             in_specs=[pl.BlockSpec(memory_space=pltpu.SMEM)] + [pl.BlockSpec(memory_space=pl.ANY)] * 10,
-            out_specs=pl.BlockSpec(memory_space=vmem),
+            out_specs=pl.BlockSpec(memory_space=pl.ANY),
             scratch_shapes=[
                 vmem((1, nc * cols), jnp.int32),
                 vmem((area, ch), BF16),
@@ -456,10 +461,10 @@
                 vmem((per, devs, 2 * rows, cols), BF16),
                 vmem((2, per, devs, rows, cols), BF16),
                 vmem((2, per, devs, rows, cols), BF16),
-                vmem((2, nc, nz, rows, cols), BF16),
-                vmem((2, devs, rows, cols), BF16),
-                vmem((2, 2, nc, nz, rows // 2, cols), BF16),
-                vmem((2, 2, devs, rows // 2, cols), BF16),
+                vmem((3, nc, nz, rows, cols), BF16),
+                vmem((3, devs, rows, cols), BF16),
+                vmem((2, nc, nz, rows // 2, cols), BF16),
+                vmem((2, devs, rows // 2, cols), BF16),
                 vmem((nc, area, ch), BF16),
                 vmem((HEADS * rows, cols), F32),
                 vmem((HEADS * rows, cols), BF16),
@@ -468,14 +473,17 @@
                 vmem((rows, nc * cols, HEADS * cols), F32),
                 vmem((rows, ch, nc * cols), BF16),
                 vmem((rows, ch, cols), F32),
-                pltpu.SemaphoreType.REGULAR((2, 4)),
+                vmem((rows, cols, ch), BF16),
+                pltpu.SemaphoreType.REGULAR((2, 2)),
                 pltpu.SemaphoreType.DMA((2, per)),
                 pltpu.SemaphoreType.DMA((2, 2, per)),
+                pltpu.SemaphoreType.DMA((2, 3)),
                 pltpu.SemaphoreType.DMA((2, 2)),
-                pltpu.SemaphoreType.DMA((2, 2, 2)),
                 pltpu.SemaphoreType.DMA((2,)),
-                pltpu.SemaphoreType.DMA((half // 4,)),
-                pltpu.SemaphoreType.DMA((3,)),
+                pltpu.SemaphoreType.DMA((lots,)),
+                pltpu.SemaphoreType.DMA((lots,)),
+                pltpu.SemaphoreType.DMA((2,)),
+                pltpu.SemaphoreType.DMA((rows // 2,)),
             ],
             compiler_params=pltpu.CompilerParams(
                 collective_id=1, has_side_effects=True, vmem_limit_bytes=62 * 1024 * 1024
@@ -485,7 +493,7 @@
             crop_length, residue_mask.reshape(1, nc * cols), pair_rep.reshape(area, ch), norm_gain, mult_proj,
             mixed_gain, mult_out, att_gain.reshape(1, ch), att_proj, att_bias.T, att_out,
         )
-        return out.reshape(rows, cols, ch)
+        return out
 
     return jax.shard_map(
         local,

time: 199 us -> 193 us (0.970)
  Pallas kernels: 196 us -> 191 us
    pallas_call x1, Pallas kernels: 196 us -> 191 us  [local(): pl.pallas_call(functools.partial(kernel, nz, nc, rows, stride, 4), out_sh...]
where the time goes in v4:
time: 193 us
  Pallas kernels  191 us (99%)
    pallas_call x1, Pallas kernels, local(): pl.pallas_call(functools.partial(kernel, nz, nc, rows, stride, 4), out_sh...  191 us

profile of v4, /device:TPU:46, one launch (start us, length us, event | category | flops | bytes accessed | tf_op | source)
XLA Modules:
  0.0 192.9 jit_solution(960735677106413139)
XLA Ops:
  0.7 190.6 %triangle.1 = bf16[8,128,128]{2,1,0:T(8,128)(2,1)} custom-call(s32[1]{0:T(128)S(6)} %copy.13.crop_ref, s32[1,256]{1,0:T(1,128)} %bitcast.5, bf16[1024,128]{1,0:T(8,128)(2,1)} %bitcast.4, f32[2,128]{1,0:T(2,128)} %ng_hbm.1, bf16[2,128,640]{2,1,0:T(8,128)(2,1)} %mp_hbm.1, f32[2,128]{1,0:T(2,128)} %mg_hbm.1, bf16[2,128,128]{2,1,0:T(8,128)(2,1)} %mo_hbm.1, ...), custom_call_target="tpu_custom_call" | custom-call | tf_op jit(solution)/shard_map/triangle/pallas_call | solution.py:432
  191.2 1.7 copy.14

commit v5 on v4

--- a/solution.py
+++ b/solution.py
@@ -9,6 +9,7 @@
 
 HEADS = 4
 EPSILON = 1e-05
+LOG2E = 1.4426950408889634
 MESH = pl.DeviceIdType.MESH
 F32 = jnp.float32
 BF16 = jnp.bfloat16
@@ -238,7 +239,7 @@
     def first_row(r):
         project(0, r)
 
-    rows_loop(first_row)
+    rows_loop(first_row, step=4)
     pl.semaphore_wait(barrier, (2 * reach) * nc + 1)
     tell(reach, 0)
     pack(0)
@@ -271,7 +272,7 @@
             updated(0, r)
             project(1, r, hf)
 
-        rows_loop(both_steps, hf * hr, (hf + 1) * hr)
+        rows_loop(both_steps, hf * hr, (hf + 1) * hr, step=4)
         for k in range(per):
             send_second(hf, k)
     rows_loop(functools.partial(gate_row, 1))
@@ -334,7 +335,7 @@
             if h < HEADS - 1:
                 parts.append(jnp.zeros(((HEADS - 1 - h) * hd, cols), BF16))
             wide.append(jnp.concatenate(parts, axis=0))
-        sc[r] = dot(keys, jnp.concatenate(wide, axis=1), NN) * (1.0 / float(hd) ** 0.5)
+        sc[r] = dot(keys, jnp.concatenate(wide, axis=1), NN) * (LOG2E / float(hd) ** 0.5)
 
     swap.wait()
     rows_loop(scores_row)
@@ -367,13 +368,13 @@
         for h in range(HEADS):
             tile = jnp.stack([p[:, h * rows:(h + 1) * rows] for p in part], axis=1).reshape(half * rows, cols)
             tile = tile + km_ref[:, kc * cols:(kc + 1) * cols]
-            bt[kc * cols:(kc + 1) * cols, h * cols:(h + 1) * cols] = jnp.transpose(tile)
+            bt[kc * cols:(kc + 1) * cols, h * cols:(h + 1) * cols] = jnp.transpose(tile * LOG2E)
 
     def attend_row(r):
         sl = pl.ds(pl.multiple_of(r * cols, cols), cols)
         score = sc[r] + bt[...]
         top = jnp.max(score, axis=0, keepdims=True)
-        e = jnp.exp(score - top)
+        e = jnp.exp2(score - top)
         inv = 1.0 / jnp.sum(e, axis=0, keepdims=True)
         got = dot(vt[r], e.astype(BF16), NN)
         parts = []
@@ -383,17 +384,19 @@
         gated = (sg[r] * jnp.concatenate(parts, axis=0)).astype(BF16)
         ob[r] = (zb[sl, :].astype(F32) + dot(gated, ao_ref[...], TN)).astype(BF16)
 
+    at_once = 4
+
     def leave(i):
-        some = pl.ds(i * 2, 2)
+        some = pl.ds(i * at_once, at_once)
         return pltpu.make_async_copy(ob.at[some], out_hbm.at[some], sem_o.at[i])
 
-    def two_rows(i, carry):
-        attend_row(2 * i)
-        attend_row(2 * i + 1)
+    def some_rows(i, carry):
+        for t in range(at_once):
+            attend_row(at_once * i + t)
         leave(i).start()
         return carry
 
-    lax.fori_loop(0, rows // 2, two_rows, 0)
+    lax.fori_loop(0, rows // at_once, some_rows, 0)
 
     for k in range(per):
         landed(r_lr.at[k], sem_lr.at[0, k], sem_lr.at[1, k]).wait_send()
@@ -412,7 +415,7 @@
         bias_wait(hops, sem_b.at[0], sem_bf.at[0]).wait_send()
 
     bias_wait(len(near) * many, sem_b.at[1], sem_bf.at[0]).wait_send()
-    for i in range(rows // 2):
+    for i in range(rows // at_once):
         leave(i).wait()
 
 

time: 193 us -> 194 us (level); the launches traced: 193 us -> 192 us
  Pallas kernels: 191 us -> 189 us
where the time goes in v5:
time: 194 us; the launch traced here: 192 us
  Pallas kernels  189 us (97%)
    pallas_call x1, Pallas kernels, local(): pl.pallas_call(functools.partial(kernel, nz, nc, rows, stride, 4), out_sh...  189 us

profile of v5, /device:TPU:46, one launch (start us, length us, event | category | flops | bytes accessed | tf_op | source)
XLA Modules:
  0.0 191.8 jit_solution(13600811899744083120)
XLA Ops:
  0.7 189.5 %triangle.1 = bf16[8,128,128]{2,1,0:T(8,128)(2,1)} custom-call(s32[1]{0:T(128)S(6)} %copy.13.crop_ref, s32[1,256]{1,0:T(1,128)} %bitcast.5, bf16[1024,128]{1,0:T(8,128)(2,1)} %bitcast.4, f32[2,128]{1,0:T(2,128)} %ng_hbm.1, bf16[2,128,640]{2,1,0:T(8,128)(2,1)} %mp_hbm.1, f32[2,128]{1,0:T(2,128)} %mg_hbm.1, bf16[2,128,128]{2,1,0:T(8,128)(2,1)} %mo_hbm.1, ...), custom_call_target="tpu_custom_call" | custom-call | tf_op jit(solution)/shard_map/triangle/pallas_call | solution.py:435
  190.1 1.7 copy.14

commit v6 on v5

--- a/solution.py
+++ b/solution.py
@@ -239,7 +239,7 @@
     def first_row(r):
         project(0, r)
 
-    rows_loop(first_row, step=4)
+    rows_loop(first_row)
     pl.semaphore_wait(barrier, (2 * reach) * nc + 1)
     tell(reach, 0)
     pack(0)
@@ -272,7 +272,7 @@
             updated(0, r)
             project(1, r, hf)
 
-        rows_loop(both_steps, hf * hr, (hf + 1) * hr, step=4)
+        rows_loop(both_steps, hf * hr, (hf + 1) * hr)
         for k in range(per):
             send_second(hf, k)
     rows_loop(functools.partial(gate_row, 1))
@@ -340,6 +340,14 @@
     swap.wait()
     rows_loop(scores_row)
 
+    for k in range(per):
+        landed(r_lr.at[k], sem_lr.at[0, k], sem_lr.at[1, k]).wait_send()
+        landed(r_q.at[k], sem_q.at[0, k], sem_q.at[1, k]).wait_send()
+        for hf in range(2):
+            landed(r_l2.at[hf, k], sem_l2.at[0, hf, k], sem_l2.at[1, hf, k]).wait_send()
+    for n in range(3):
+        landed(r_p.at[n], sem_p.at[0, n], sem_p.at[1, n]).wait_send()
+
     ahead = lax.rem(z + nz - c * half, nz)
     rising = (ahead < half // 2) | (ahead >= nz - half // 2)
     order = [jnp.where(rising, i, lots - 1 - i) for i in range(lots)]
@@ -361,6 +369,15 @@
 
     for m in order:
         bias_wait(len(near) * nc, sem_b.at[1], sem_bs.at[m]).wait_recv()
+    @pl.when(to == c)
+    def _():
+        bias_wait(hops - 1, sem_b.at[0], sem_bf.at[0]).wait_send()
+
+    @pl.when(to != c)
+    def _():
+        bias_wait(hops, sem_b.at[0], sem_bf.at[0]).wait_send()
+
+    bias_wait(len(near) * many, sem_b.at[1], sem_bf.at[0]).wait_send()
     for kc in range(nc):
         part = [
             jnp.stack([r_b[q * many + m * nc + kc] for m in range(lots)]).astype(F32) for q in range(stride)
@@ -398,23 +415,6 @@
 
     lax.fori_loop(0, rows // at_once, some_rows, 0)
 
-    for k in range(per):
-        landed(r_lr.at[k], sem_lr.at[0, k], sem_lr.at[1, k]).wait_send()
-        landed(r_q.at[k], sem_q.at[0, k], sem_q.at[1, k]).wait_send()
-        for hf in range(2):
-            landed(r_l2.at[hf, k], sem_l2.at[0, hf, k], sem_l2.at[1, hf, k]).wait_send()
-    for n in range(3):
-        landed(r_p.at[n], sem_p.at[0, n], sem_p.at[1, n]).wait_send()
-
-    @pl.when(to == c)
-    def _():
-        bias_wait(hops - 1, sem_b.at[0], sem_bf.at[0]).wait_send()
-
-    @pl.when(to != c)
-    def _():
-        bias_wait(hops, sem_b.at[0], sem_bf.at[0]).wait_send()
-
-    bias_wait(len(near) * many, sem_b.at[1], sem_bf.at[0]).wait_send()
     for i in range(rows // at_once):
         leave(i).wait()
 

time: 194 us -> 193 us (level)
  no operation moved by 1% of the time
where the time goes in v6:
time: 193 us; the launch traced here: 192 us
  Pallas kernels  190 us (98%)
    pallas_call x1, Pallas kernels, local(): pl.pallas_call(functools.partial(kernel, nz, nc, rows, stride, 4), out_sh...  190 us

profile of v6, /device:TPU:46, one launch (start us, length us, event | category | flops | bytes accessed | tf_op | source)
XLA Modules:
  0.0 192.4 jit_solution(18134228272572738926)
XLA Ops:
  0.7 190.0 %triangle.1 = bf16[8,128,128]{2,1,0:T(8,128)(2,1)} custom-call(s32[1]{0:T(128)S(6)} %copy.13.crop_ref, s32[1,256]{1,0:T(1,128)} %bitcast.5, bf16[1024,128]{1,0:T(8,128)(2,1)} %bitcast.4, f32[2,128]{1,0:T(2,128)} %ng_hbm.1, bf16[2,128,640]{2,1,0:T(8,128)(2,1)} %mp_hbm.1, f32[2,128]{1,0:T(2,128)} %mg_hbm.1, bf16[2,128,128]{2,1,0:T(8,128)(2,1)} %mo_hbm.1, ...), custom_call_target="tpu_custom_call" | custom-call | tf_op jit(solution)/shard_map/triangle/pallas_call | solution.py:435
  190.7 1.7 copy.14

commit v7 on v6

--- a/solution.py
+++ b/solution.py
@@ -121,7 +121,7 @@
     col_alive = alive[:, :cols]
     for cc in range(1, nc):
         col_alive = jnp.where(c == cc, alive[:, cc * cols:(cc + 1) * cols], col_alive)
-    pm_ref[...] = row_alive * col_alive
+    pm_ref[:rows, :] = row_alive * col_alive
 
     def by_channel(u):
         for q in range(4):
@@ -293,7 +293,7 @@
         normed_row(r)
 
     rows_loop(last_steps, step=4)
-    s_b[...] = fb[...].astype(BF16)
+    s_b[...] = fb[:HEADS * rows, :].astype(BF16)
     to = z // half
     lots = half // stride
     many = nc * lots
@@ -449,7 +449,7 @@
                 vmem((HEADS, ch), BF16),
                 vmem(att_out.shape, BF16),
                 pltpu.SemaphoreType.DMA((10,)),
-                vmem((rows, cols), F32),
+                vmem((2 * rows, cols), F32),
                 vmem((1, nc * cols), F32),
                 vmem((2, 4 * ch, ch), BF16),
                 vmem((2, ch, ch), F32),
@@ -469,7 +469,7 @@
                 vmem((2, nc, nz, rows // 2, cols), BF16),
                 vmem((2, devs, rows // 2, cols), BF16),
                 vmem((nc, area, ch), BF16),
-                vmem((HEADS * rows, cols), F32),
+                vmem((8 * rows, cols), F32),
                 vmem((HEADS * rows, cols), BF16),
                 vmem((nc * half, HEADS * rows, cols), BF16),
                 vmem((nc * cols, HEADS * cols), F32),

time: 193 us -> 193 us (level)
  no operation moved by 1% of the time
where the time goes in v7:
time: 193 us; the launch traced here: 192 us
  Pallas kernels  190 us (98%)
    pallas_call x1, Pallas kernels, local(): pl.pallas_call(functools.partial(kernel, nz, nc, rows, stride, 4), out_sh...  190 us

profile of v7, /device:TPU:46, one launch (start us, length us, event | category | flops | bytes accessed | tf_op | source)
XLA Modules:
  0.0 192.5 jit_solution(16707677412828967030)
XLA Ops:
  0.7 190.1 %triangle.1 = bf16[8,128,128]{2,1,0:T(8,128)(2,1)} custom-call(s32[1]{0:T(128)S(6)} %copy.13.crop_ref, s32[1,256]{1,0:T(1,128)} %bitcast.5, bf16[1024,128]{1,0:T(8,128)(2,1)} %bitcast.4, f32[2,128]{1,0:T(2,128)} %ng_hbm.1, bf16[2,128,640]{2,1,0:T(8,128)(2,1)} %mp_hbm.1, f32[2,128]{1,0:T(2,128)} %mg_hbm.1, bf16[2,128,128]{2,1,0:T(8,128)(2,1)} %mo_hbm.1, ...), custom_call_target="tpu_custom_call" | custom-call | tf_op jit(solution)/shard_map/triangle/pallas_call | solution.py:435
  190.8 1.7 copy.14
